TPU v7x, 32 devices: a whole 2x2x4 slice. The times are simulated.
32 devices in a mesh: prompt: 4 (over y, x), resp: 8 (over z, core).
Axes of the slice: x: 2, y: 2, z: 4, core: 2. Of those that a mesh axis runs over, the one named last changes fastest.
Arguments:
- embeddings: bfloat16 [32, 256, 3584], P('prompt', 'resp'), parts along dimension 0, may hold values from -6 to 6
- head_weight: bfloat16 [3584, 3584], P('resp'), may hold values from -0.0017089844 to 0.0017089844
- valid_mask: int32 [32, 256], P('prompt', 'resp'), parts along dimension 0, may hold values from 0 to 1, as said below
Outputs:
- preferences: float32 [32, 256, 256], P('prompt', 'resp'), parts along dimension 0
- win_rates: float32 [32, 256], P('prompt', 'resp'), parts along dimension 0
There are 4 independent parts, one for each index of `prompt`. A program takes and returns all parts, laid end to end along the dimension named above; an argument that names none is the same for every part. Nothing has to cross between parts.
Inputs may be any that keep to these rules, and one draw needn't show every extreme that they name: `valid_mask`: for each prompt the ones are its first response slots, between 64 and 256 of them; in every draw some prompt has all 256 slots filled.
All inputs are finite; a program needn't handle non-finite values.
Results may differ from a plain program's by a relative error of at most 0.003.
Values may be sent and summed in bfloat16 or wider, within the bound.
A program may use at most 128 MiB of HBM per device.

v0:
```python
import functools

import jax
import jax.numpy as jnp
from jax import lax
from jax.experimental import pallas as pl
from jax.experimental.pallas import tpu as pltpu
from jax.sharding import PartitionSpec as P

MESH = pl.DeviceIdType.MESH
CORES = 2
CHIPS = 4
PARTS = 4
NT = (((1,), (1,)), ((), ()))


def gathered_halves(embeddings, head_weight, own_index, group_size):
    prompts, block_rows, features = embeddings.shape
    held = head_weight.shape[0]
    slots = group_size * block_rows
    everyone = lax.all_gather(embeddings, "resp", axis=0, tiled=True)
    flat = everyone.reshape(group_size * prompts * block_rows, features)
    through = lax.dot_general(flat, head_weight, NT, preferred_element_type=jnp.float32)
    through = through.astype(jnp.bfloat16).reshape(group_size, prompts, block_rows, held)
    mine = lax.dynamic_slice_in_dim(
        everyone.reshape(group_size, prompts, block_rows, features), own_index * held, held, 3
    )
    partial = jnp.einsum("gpid,hpjd->gpihj", mine, through, preferred_element_type=jnp.float32)
    flipped = jnp.einsum("gpid,hpjd->gpihj", through, mine, preferred_element_type=jnp.float32)
    partial = (partial - flipped).astype(jnp.bfloat16)
    return partial.reshape(group_size, prompts, block_rows, slots)


def gathered_scores(embeddings, head_weight):
    group_size = lax.axis_size("resp")
    own_index = lax.axis_index("resp")
    prompts, block_rows, features = embeddings.shape
    slots = group_size * block_rows
    at_once = max(1, min(prompts, (1 << 11) // slots))

    def scores_of(some):
        partial = gathered_halves(some, head_weight, own_index, group_size)
        swapped = lax.all_to_all(partial, "resp", split_axis=0, concat_axis=0, tiled=True)
        return jnp.sum(swapped.astype(jnp.float32), axis=0)

    pieces = embeddings.reshape(prompts // at_once, at_once, block_rows, features)
    return lax.map(scores_of, pieces).reshape(prompts, block_rows, slots)


def kernel(e_ref, w_ref, m_ref, o_ref, r_ref,
           ebuf, wbuf, zbuf, sbuf, keep, pbuf, qbuf, fbuf, rbuf, mine_cols, mbuf,
           m_send, m_recv, e_send, e_recv, ef_send, el_sem,
           w_send, w_recv, a_send, a_recv, wl_sem, p_send, p_recv, f_send, r_recv):
    part = lax.axis_index("prompt")
    me = lax.axis_index("resp")
    z = me // CORES
    core = me % CORES
    half = z // 2
    prompts, block_rows, features = e_ref.shape
    held = w_ref.shape[0]
    per_core = prompts // CORES
    group = CHIPS * CORES
    span = held * group // 2
    rows = group * block_rows
    half_rows = rows // 2
    z_in = 1 + half
    z_out = 3 * half
    z_far = 2 - half
    far_out = 3 - z_out
    inner = z == z_in
    quarter = held // PARTS
    width = 256 if span % 256 == 0 else span

    def copy(src, dst, send, recv, chip, c, q=None):
        return pltpu.make_async_remote_copy(
            src, dst, send, recv,
            device_id=(part if q is None else q, chip * CORES + c), device_id_type=MESH,
        )

    def arrived(dst, recv):
        copy(dst, dst, m_send.at[0], recv, z_far, core).wait_recv()

    valid = m_ref[...].astype(jnp.float32)
    slot = lax.broadcasted_iota(jnp.int32, (block_rows, rows), 1) - me * block_rows
    place = (slot == lax.broadcasted_iota(jnp.int32, (block_rows, rows), 0)).astype(jnp.float32)
    mine_cols[...] = jnp.dot(valid, place, preferred_element_type=jnp.float32).astype(jnp.int32)

    others = [lax.rem(me + d, group) for d in range(1, group)]
    plane = [lax.rem(part + d, PARTS) for d in range(1, PARTS)]
    barrier = pltpu.get_barrier_semaphore()
    for other in others:
        pl.semaphore_signal(barrier, inc=1, device_id=(part, other), device_id_type=MESH)
    for q in plane:
        pl.semaphore_signal(barrier, inc=1, device_id=(q, me), device_id_type=MESH)
    pl.semaphore_wait(barrier, len(others) + len(plane))

    def w_rows(block, start, size):
        return wbuf.at[pl.ds(pl.multiple_of(block * held + start, 16), size)]

    def mask_copy(d):
        return pltpu.make_async_remote_copy(
            mine_cols, mbuf.at[me], m_send.at[d], m_recv.at[me],
            device_id=(part, others[d]), device_id_type=MESH,
        )

    my_block = me - half * group // 2
    out_block = z_out * CORES + core - half * group // 2
    out_other = z_out * CORES + 1 - core - half * group // 2
    in_other = z_in * CORES + 1 - core - half * group // 2
    my_quarter = pl.multiple_of(part * quarter, 16)
    first = quarter // 32 * 16
    pieces = ((0, first), (first, quarter - first))

    def outer_w(i):
        at, size = pieces[i]
        return copy(w_ref.at[pl.ds(pl.multiple_of(my_quarter + at, 16), size)],
                    w_rows(my_block, my_quarter + at, size),
                    w_send.at[0, i], w_recv.at[part, i], z_in, core)

    def outer_e(j, c):
        return copy(e_ref.at[c * per_core + j], ebuf.at[j, me],
                    e_send.at[j, c], e_recv.at[j, me], z_in, c)

    def far_e(j, c):
        return copy(e_ref.at[c * per_core + j], ebuf.at[j, me],
                    e_send.at[j, c], e_recv.at[j, me], z_far, c)

    def near_e(j):
        return copy(e_ref.at[(1 - core) * per_core + j], ebuf.at[j, me],
                    e_send.at[j, 2], e_recv.at[j, me], z_in, 1 - core)

    def own_e(j):
        return pltpu.make_async_copy(e_ref.at[core * per_core + j], ebuf.at[j, me], el_sem.at[j])

    def onward_e(j, c):
        spot = ebuf.at[j, z_out * CORES + c]
        return copy(spot, spot, ef_send.at[j, c], e_recv.at[j, z_out * CORES + c], z_far, core)

    def near_w():
        return copy(w_ref, w_rows(my_block, 0, held), w_send.at[0, 0], w_recv.at[PARTS, 0], z_in, 1 - core)

    def own_w():
        return pltpu.make_async_copy(w_ref, w_rows(my_block, 0, held), wl_sem.at[0])

    def plane_w(d, i):
        at, size = pieces[i]
        spot = w_rows(out_block, my_quarter + at, size)
        return copy(spot, spot, w_send.at[1 + d, i], w_recv.at[part, i], z_in, core, plane[d])

    def across_w(q, i):
        at, size = pieces[i]
        spot = w_rows(out_block, q * quarter + at, size)
        return copy(spot, spot, a_send.at[q, i], a_recv.at[q, i], z_in, 1 - core)

    def partial_copy(j):
        return copy(pbuf.at[j], qbuf.at[j], p_send.at[j], p_recv.at[j], z_far, core)

    def final_copy(j, t):
        target = half * (group // 2) + lax.rem(my_block + 1 + t, group // 2)
        row = pl.multiple_of(lax.rem(my_block + 1 + t, group // 2) * block_rows, block_rows)
        return pltpu.make_async_remote_copy(
            fbuf.at[j, pl.ds(row, block_rows)], rbuf.at[core * per_core + j],
            f_send.at[j, t], r_recv.at[core * per_core + j],
            device_id=(part, target), device_id_type=MESH,
        )

    @pl.when(jnp.logical_not(inner))
    def _():
        for i in range(2):
            outer_w(i).start()
        for j in range(per_core):
            for c in range(CORES):
                outer_e(j, c).start()

    @pl.when(inner)
    def _():
        for j in range(per_core):
            for c in range(CORES):
                far_e(j, c).start()
        near_w().start()
        for j in range(per_core):
            near_e(j).start()
        own_w().start()
        for j in range(per_core):
            own_e(j).start()

    for d in range(group - 1):
        mask_copy(d).start()
    mbuf[me] = mine_cols[...]

    @pl.when(inner)
    def _():
        def pass_on(j, carry):
            for c in range(CORES):
                arrived(ebuf.at[j, z_out * CORES + c], e_recv.at[j, z_out * CORES + c])
                onward_e(j, c).start()
            return carry

        for i in range(2):
            at, size = pieces[i]
            arrived(w_rows(out_block, my_quarter + at, size), w_recv.at[part, i])
            for d in range(PARTS - 1):
                plane_w(d, i).start()
            across_w(part, i).start()
        lax.fori_loop(0, per_core // 2, pass_on, 0)
        for i in range(2):
            at, size = pieces[i]
            for q in plane:
                arrived(w_rows(out_block, q * quarter + at, size), w_recv.at[q, i])
                across_w(q, i).start()
        own_w().wait()
        arrived(w_rows(in_other, 0, held), w_recv.at[PARTS, 0])
        lax.fori_loop(per_core // 2, per_core - 1, pass_on, 0)
        for i in range(2):
            at, size = pieces[i]
            for q in range(PARTS):
                arrived(w_rows(out_other, q * quarter + at, size), a_recv.at[q, i])

        mine_at = pl.multiple_of(half * half_rows, half_rows)
        theirs_at = pl.multiple_of((1 - half) * half_rows, half_rows)
        lanes = pl.ds(pl.multiple_of(half * span, 128), span)

        def finish(j):
            arrived(qbuf.at[j], p_recv.at[j])
            fbuf[j] = (keep[j] + qbuf[j].astype(jnp.float32)).astype(jnp.bfloat16)
            for t in range(group // 2 - 1):
                final_copy(j, t).start()
            own_row = pl.multiple_of(my_block * block_rows, block_rows)
            rbuf[core * per_core + j] = fbuf[j, pl.ds(own_row, block_rows)]

        def project(j, many, block, blocks):
            row = pl.multiple_of(block * block_rows, block_rows)
            tall = blocks * block_rows

            def chunk(k, inside):
                start = pl.multiple_of(k * width, width)
                left = ebuf[pl.ds(j, many), pl.ds(block, blocks)].reshape(many * tall, features)
                zbuf[pl.ds(j, many), pl.ds(row, tall), pl.ds(start, width)] = lax.dot_general(
                    left, wbuf[pl.ds(start, width)], NT, preferred_element_type=jnp.float32
                ).astype(jnp.bfloat16).reshape(many, tall, width)
                return inside

            lax.fori_loop(0, span // width, chunk, 0)

        pair = per_core // 2

        def early(n, carry):
            @pl.when(n == 1)
            def _():
                pass_on(per_core - 1, 0)

            for i in range(pair):
                j = n * pair + i
                own_e(j).wait()
                arrived(ebuf.at[j, z_in * CORES + 1 - core], e_recv.at[j, z_in * CORES + 1 - core])
                for c in range(CORES):
                    arrived(ebuf.at[j, z_far * CORES + c], e_recv.at[j, z_far * CORES + c])
            project(n * pair, pair, half * CORES, group - CORES)
            return carry

        lax.fori_loop(0, 2, early, 0)

        def last_rows(j, carry):
            for c in range(CORES):
                arrived(ebuf.at[j, far_out * CORES + c], e_recv.at[j, far_out * CORES + c])
            return carry

        lax.fori_loop(0, per_core - 1, last_rows, 0)
        project(0, per_core - 1, far_out * CORES, CORES)

        def score(j, carry):
            @pl.when(j == per_core - 1)
            def _():
                last_rows(per_core - 1, 0)
                project(per_core - 1, 1, far_out * CORES, CORES)

            left = ebuf[j, :, :, lanes].reshape(rows, span)
            right = zbuf[j]
            sbuf[...] = lax.dot_general(
                left, right, NT, preferred_element_type=jnp.float32
            ) - lax.dot_general(right, left, NT, preferred_element_type=jnp.float32)
            pbuf[j] = sbuf[pl.ds(theirs_at, half_rows)].astype(jnp.bfloat16)
            partial_copy(j).start()
            keep[j] = sbuf[pl.ds(mine_at, half_rows)]
            return carry

        lax.fori_loop(0, per_core, score, 0)
        for j in range(per_core):
            finish(j)
        for j in range(per_core):
            arrived(rbuf.at[(1 - core) * per_core + j], r_recv.at[(1 - core) * per_core + j])
        for j in range(per_core):
            for c in range(CORES):
                far_e(j, c).wait_send()
                onward_e(j, c).wait_send()
            near_e(j).wait_send()
            partial_copy(j).wait_send()
            for t in range(group // 2 - 1):
                final_copy(j, t).wait_send()
        near_w().wait_send()
        for i in range(2):
            for q in range(PARTS):
                across_w(q, i).wait_send()
        for d in range(PARTS - 1):
            for i in range(2):
                plane_w(d, i).wait_send()

    @pl.when(jnp.logical_not(inner))
    def _():
        for i in range(2):
            outer_w(i).wait_send()
        for j in range(per_core):
            for c in range(CORES):
                outer_e(j, c).wait_send()
        for p in range(prompts):
            arrived(rbuf.at[p], r_recv.at[p])

    for d in range(group - 1):
        mask_copy(d).wait_send()
        arrived(mbuf.at[others[d]], m_recv.at[others[d]])
    cols = mbuf[0]
    for g in range(1, group):
        cols = cols + mbuf[g]
    cols = cols.astype(jnp.float32)
    counts = jnp.sum(cols, axis=1, keepdims=True)
    pairs = jnp.maximum(counts - 1.0, 1.0)
    same = lax.broadcasted_iota(jnp.int32, (block_rows, block_rows), 0)
    same = (same == lax.broadcasted_iota(jnp.int32, (block_rows, block_rows), 1)).astype(jnp.float32)
    down = lax.dot_general(same, valid, NT, preferred_element_type=jnp.float32)
    lane = lax.broadcasted_iota(jnp.int32, (block_rows, 128), 1)
    rates = jnp.zeros((block_rows, 128), jnp.float32)
    for p in range(prompts):
        here = down[:, p:p + 1]
        prefs = jax.nn.sigmoid(rbuf[p].astype(jnp.float32)) * here * cols[p:p + 1, :]
        o_ref[p] = prefs
        totals = jnp.sum(prefs, axis=1, keepdims=True) - 0.5 * here
        rates = jnp.where(lane == p, here * totals / pairs[p:p + 1, :], rates)
    r_ref[...] = jnp.transpose(rates)[:prompts]


def line_scores(embeddings, head_weight, mask):
    prompts, block_rows, features = embeddings.shape
    held = head_weight.shape[0]
    group = CHIPS * CORES
    per_core = prompts // CORES
    span = held * group // 2
    rows = group * block_rows
    half_rows = rows // 2
    bf16, f32 = jnp.bfloat16, jnp.float32
    dma = pltpu.SemaphoreType.DMA
    anywhere = pl.BlockSpec(memory_space=pl.ANY)
    vmem = pl.BlockSpec(memory_space=pltpu.VMEM)
    return pl.pallas_call(
        kernel,
        out_shape=(
            jax.ShapeDtypeStruct((prompts, block_rows, rows), f32),
            jax.ShapeDtypeStruct((prompts, block_rows), f32),
        ),
        in_specs=[anywhere, anywhere, vmem],
        out_specs=(vmem, vmem),
        scratch_shapes=[
            pltpu.VMEM((per_core, group, block_rows, features), bf16),
            pltpu.VMEM((span, features), bf16),
            pltpu.VMEM((per_core, rows, span), bf16),
            pltpu.VMEM((rows, rows), f32),
            pltpu.VMEM((per_core, half_rows, rows), f32),
            pltpu.VMEM((per_core, half_rows, rows), bf16),
            pltpu.VMEM((per_core, half_rows, rows), bf16),
            pltpu.VMEM((per_core, half_rows, rows), bf16),
            pltpu.VMEM((prompts, block_rows, rows), bf16),
            pltpu.VMEM((prompts, rows), jnp.int32),
            pltpu.VMEM((group, prompts, rows), jnp.int32),
            dma((group - 1,)),
            dma((group,)),
            dma((per_core, 3)),
            dma((per_core, group)),
            dma((per_core, CORES)),
            dma((per_core,)),
            dma((PARTS, 2)),
            dma((PARTS + 1, 1 + 1)),
            dma((PARTS, 2)),
            dma((PARTS, 2)),
            dma((1,)),
            dma((per_core,)),
            dma((per_core,)),
            dma((per_core, group // 2 - 1)),
            dma((prompts,)),
        ],
        compiler_params=pltpu.CompilerParams(
            collective_id=0, has_side_effects=True, vmem_limit_bytes=56 << 20
        ),
    )(embeddings, head_weight, mask)


def shards(embeddings, head_weight, valid_mask):
    group_size = lax.axis_size("resp")
    slots = group_size * embeddings.shape[1]
    if (lax.axis_size("prompt"), group_size) == (PARTS, CHIPS * CORES):
        return line_scores(embeddings, head_weight, valid_mask)
    valid_rows = valid_mask.astype(jnp.float32)
    counts = lax.psum(jnp.sum(valid_rows, axis=1), "resp")
    scores = gathered_scores(embeddings, head_weight)
    column_ids = jnp.arange(slots, dtype=jnp.float32)
    valid_cols = (column_ids[None, :] < counts[:, None]).astype(jnp.float32)
    preferences = jax.nn.sigmoid(scores) * valid_rows[:, :, None] * valid_cols[:, None, :]
    totals = jnp.sum(preferences, axis=2) - 0.5 * valid_rows
    win_rates = valid_rows * totals / jnp.maximum(counts - 1.0, 1.0)[:, None]
    return (preferences, win_rates)


def solution(mesh):
    return jax.shard_map(
        shards,
        mesh=mesh,
        in_specs=(P("prompt", "resp", None), P("resp", None), P("prompt", "resp")),
        out_specs=(P("prompt", "resp", None), P("prompt", "resp")),
        check_vma=False,
    )
```

profile of v0, /device:TPU:0, one launch (start us, length us, event | category | flops | bytes accessed | tf_op | source)
XLA Modules:
  0.0 105.5 jit_solution(12897419995467779145)
XLA Ops:
  0.6 102.0 %shard_map.50 = (f32[8,32,256]{2,1,0:T(8,128)}, f32[8,32]{1,0:T(8,128)}) custom-call(bf16[8,32,3584]{2,1,0:T(8,128)(2,1)} %e_ref.1, bf16[448,3584]{1,0:T(8,128)(2,1)} %w_ref.1, s32[8,32]{1,0:T(8,128)} %m_ref.1), custom_call_target="tpu_custom_call" | custom-call | tf_op jit(solution)/shard_map/pallas_call | solution.py:353
  102.6 1.7 %copy.7 = f32[8,32,256]{2,1,0:T(8,128)} copy(f32[8,32,256]{2,1,0:T(8,128)} %get-tuple-element.4) | data formatting | bytes 524288
  104.3 1.3 %copy.8 = f32[8,32]{1,0:T(8,128)} copy(f32[8,32]{1,0:T(8,128)} %get-tuple-element.5) | data formatting | bytes 2048
where the time goes:
time: 106 us
  Pallas kernels  102 us (96%)
  local copies, waits for them, and re-layouts  2.95 us (3%)
    pallas_call x1, Pallas kernels, line_scores(): pl.pallas_call(kernel, out_shape=(jax.ShapeDtypeStruct((prompts, block_ro...  102 us
    unnamed x2, local copies, waits for them, and re-layouts  2.95 us

commit v1 on v0

v1 whole, which is shorter than its diff:
```python
import functools

import jax
import jax.numpy as jnp
from jax import lax
from jax.experimental import pallas as pl
from jax.experimental.pallas import tpu as pltpu
from jax.sharding import PartitionSpec as P

MESH = pl.DeviceIdType.MESH
CORES = 2
CHIPS = 4
PARTS = 4
NT = (((1,), (1,)), ((), ()))


def gathered_halves(embeddings, head_weight, own_index, group_size):
    prompts, block_rows, features = embeddings.shape
    held = head_weight.shape[0]
    slots = group_size * block_rows
    everyone = lax.all_gather(embeddings, "resp", axis=0, tiled=True)
    flat = everyone.reshape(group_size * prompts * block_rows, features)
    through = lax.dot_general(flat, head_weight, NT, preferred_element_type=jnp.float32)
    through = through.astype(jnp.bfloat16).reshape(group_size, prompts, block_rows, held)
    mine = lax.dynamic_slice_in_dim(
        everyone.reshape(group_size, prompts, block_rows, features), own_index * held, held, 3
    )
    partial = jnp.einsum("gpid,hpjd->gpihj", mine, through, preferred_element_type=jnp.float32)
    flipped = jnp.einsum("gpid,hpjd->gpihj", through, mine, preferred_element_type=jnp.float32)
    partial = (partial - flipped).astype(jnp.bfloat16)
    return partial.reshape(group_size, prompts, block_rows, slots)


def gathered_scores(embeddings, head_weight):
    group_size = lax.axis_size("resp")
    own_index = lax.axis_index("resp")
    prompts, block_rows, features = embeddings.shape
    slots = group_size * block_rows
    at_once = max(1, min(prompts, (1 << 11) // slots))

    def scores_of(some):
        partial = gathered_halves(some, head_weight, own_index, group_size)
        swapped = lax.all_to_all(partial, "resp", split_axis=0, concat_axis=0, tiled=True)
        return jnp.sum(swapped.astype(jnp.float32), axis=0)

    pieces = embeddings.reshape(prompts // at_once, at_once, block_rows, features)
    return lax.map(scores_of, pieces).reshape(prompts, block_rows, slots)


def kernel(e_ref, w_ref, m_ref, o_ref, r_ref,
           ebuf, wbuf, zt, sbuf, keep, pbuf, qbuf, fbuf, rbuf, mine, mbuf,
           m_send, m_recv, e_send, e_recv, n_send, h_send, el_sem,
           o_send, d_send, f_send, nw_send, wl_sem, x_send, y_send, u_send, v_send, w_recv,
           p_send, p_recv, r_send, r_recv):
    part = lax.axis_index("prompt")
    me = lax.axis_index("resp")
    z = me // CORES
    core = me % CORES
    half = z // 2
    prompts, block_rows, features = e_ref.shape
    held = w_ref.shape[0]
    group = CHIPS * CORES
    per_half = prompts // 2
    side = group // 2
    span = held * side
    rows = group * block_rows
    half_rows = rows // 2
    quarter = held // PARTS
    z_in = 1 + half
    z_out = 3 * half
    z_far = 2 - half
    z_end = 3 - z_out
    inner = z == z_in
    near = core == half
    other = 1 - core
    first = 2 * half
    second = 2 - first
    here = me % side
    x_part = part + 1 - 2 * (part % 2)
    y_part = lax.rem(part + 2, PARTS)
    d_part = PARTS - 1 - part
    step = quarter // 7
    pieces = ((0, step), (step, 2 * step), (3 * step, 2 * step), (5 * step, 2 * step))

    def copy(src, dst, send, recv, chip, c, q=None):
        return pltpu.make_async_remote_copy(
            src, dst, send, recv,
            device_id=(part if q is None else q, chip * CORES + c), device_id_type=MESH,
        )

    def arrived(dst, recv):
        copy(dst, dst, m_send.at[0], recv, z_far, core).wait_recv()

    valid = m_ref[...].astype(jnp.float32)
    mine[...] = jnp.broadcast_to(jnp.sum(m_ref[...], axis=1, keepdims=True), mine.shape)

    others = [lax.rem(me + d, group) for d in range(1, group)]
    barrier = pltpu.get_barrier_semaphore()
    for peer in others:
        pl.semaphore_signal(barrier, inc=1, device_id=(part, peer), device_id_type=MESH)
    for q in (x_part, y_part):
        pl.semaphore_signal(barrier, inc=1, device_id=(q, me), device_id_type=MESH)
    pl.semaphore_wait(barrier, len(others) + 2)

    def mask_copy(d):
        return pltpu.make_async_remote_copy(
            mine, mbuf.at[me], m_send.at[d], m_recv.at[me],
            device_id=(part, others[d]), device_id_type=MESH,
        )

    def w_rows(block, q, i):
        at, size = pieces[i]
        return wbuf.at[block, pl.ds(pl.multiple_of(q * quarter + at, 16), size)]

    def my_rows(q, i):
        at, size = pieces[i]
        return w_ref.at[pl.ds(pl.multiple_of(q * quarter + at, 16), size)]

    def outer_w(i):
        return copy(my_rows(part, i), w_rows(here, part, i), o_send.at[i], w_recv.at[here, part, i], z_in, half)

    def outer_diag(i):
        return copy(my_rows(d_part, i), w_rows(here, d_part, i), d_send.at[i], w_recv.at[here, d_part, i], z_in, half)

    def far_w(i):
        return copy(my_rows(part, i), w_rows(here, part, i), o_send.at[i], w_recv.at[here, part, i], z_far, half)

    def near_w(i):
        at = pl.ds(i * quarter, quarter)
        return copy(w_ref.at[at], wbuf.at[here, at], nw_send.at[i], w_recv.at[here, i, 0], z_in, half)

    def own_w():
        return pltpu.make_async_copy(w_ref, wbuf.at[here], wl_sem.at[0])

    def got_w(block, q, i):
        arrived(w_rows(block, q, i), w_recv.at[block, q, i])

    def along(block, q, i, sems, chip, q_to):
        spot = w_rows(block, q, i)
        return copy(spot, spot, sems.at[block, i], w_recv.at[block, q, i], chip, core, q_to)

    def to_x(block, i):
        return along(block, part, i, x_send, z_in, x_part)

    def to_y(block, i):
        return along(block, part, i, y_send, z_in, y_part)

    def to_far(block, i):
        return along(block, part, i, u_send, z_far, part)

    def x_to_y(block, i):
        return along(block, x_part, i, v_send, z_in, y_part)

    def y_to_x(block, i):
        return along(block, y_part, i, v_send, z_in, x_part)

    def relay(block, u, i):
        return x_to_y(block, i) if (i < 2) == (u == 0) else y_to_x(block, i)

    def e_copy(h, j):
        return copy(e_ref.at[h * per_half + j], ebuf.at[j, me], e_send.at[h, j], e_recv.at[j, me], 1 + h, core)

    def e_far(j):
        return copy(e_ref.at[(1 - half) * per_half + j], ebuf.at[j, me], e_send.at[1, j], e_recv.at[j, me], z_far, core)

    def e_near(j):
        return copy(e_ref.at[half * per_half + j], ebuf.at[j, me], e_send.at[0, j], e_recv.at[j, me], z_in, core)

    def near_e(j):
        return copy(e_ref.at[half * per_half + j], ebuf.at[j, me], n_send.at[j], e_recv.at[j, me], z_in, other)

    def own_e(j):
        return pltpu.make_async_copy(e_ref.at[half * per_half + j], ebuf.at[j, me], el_sem.at[j])

    away = (z_out, z_far, z_end)

    def pass_e(j, k):
        block = away[k] * CORES + core
        spot = ebuf.at[j, block]
        return copy(spot, spot, h_send.at[j, k], e_recv.at[j, block], z_in, other)

    def take_e(j):
        for k in range(3):
            block = away[k] * CORES + core
            arrived(ebuf.at[j, block], e_recv.at[j, block])
            pass_e(j, k).start()

    def have_e(j):
        own_e(j).wait()
        for chip in (z_in,) + away:
            block = chip * CORES + other
            arrived(ebuf.at[j, block], e_recv.at[j, block])

    def partial_copy(j):
        return copy(pbuf.at[j], qbuf.at[j], p_send.at[j], p_recv.at[j], z_in, other)

    def project(q, j):
        at = pl.ds(pl.multiple_of(q * quarter, 16), quarter)
        left = wbuf[:, at].reshape(side * quarter, features)
        right = ebuf[j].reshape(rows, features)
        zt[j, :, at] = lax.dot_general(
            left, right, NT, preferred_element_type=jnp.float32
        ).astype(jnp.bfloat16).reshape(side, quarter, rows)

    lanes = pl.ds(pl.multiple_of(core * span, 128), span)
    mine_at = pl.multiple_of(core * half_rows, half_rows)
    theirs_at = pl.multiple_of(other * half_rows, half_rows)

    def score(j):
        left = ebuf[j, :, :, lanes].reshape(rows, span)
        raw = jnp.dot(left, zt[j].reshape(span, rows), preferred_element_type=jnp.float32)
        sbuf[...] = raw - jnp.transpose(raw)
        pbuf[j] = sbuf[pl.ds(theirs_at, half_rows)]
        partial_copy(j).start()
        keep[j] = sbuf[pl.ds(mine_at, half_rows)]

    def final_copy(j, t):
        row = pl.multiple_of(t * block_rows, block_rows)
        return pltpu.make_async_remote_copy(
            fbuf.at[j, pl.ds(row, block_rows)], rbuf.at[half * per_half + j],
            r_send.at[j, t], r_recv.at[half * per_half + j],
            device_id=(part, core * side + t), device_id_type=MESH,
        )

    def each_target(j, act):
        for t in range(side):
            @pl.when(core * side + t != me)
            def _():
                act(final_copy(j, t))

    def finish(j):
        arrived(qbuf.at[j], p_recv.at[j])
        fbuf[j] = (keep[j] + qbuf[j]).astype(jnp.bfloat16)
        each_target(j, lambda c: c.start())

        @pl.when(near)
        def _():
            row = pl.multiple_of(here * block_rows, block_rows)
            rbuf[half * per_half + j] = fbuf[j, pl.ds(row, block_rows)]

    def each_mask():
        for d in range(group - 1):
            mask_copy(d).start()

    def settle():
        for j in range(per_half):
            e_far(j).wait_send()
            near_e(j).wait_send()
            for k in range(3):
                pass_e(j, k).wait_send()
            partial_copy(j).wait_send()
            each_target(j, lambda c: c.wait_send())
        for i in range(len(pieces)):
            far_w(i).wait_send()

    def loop(n, body):
        def run(j, carry):
            body(j)
            return carry
        lax.fori_loop(0, n, run, 0)

    def all_quarters(j):
        loop(PARTS, lambda q: project(q, j))

    @pl.when(jnp.logical_not(inner))
    def _():
        for i in range(len(pieces)):
            outer_w(i).start()
        for j in range(per_half):
            e_far(j).start()
            e_near(j).start()
            if j == 0:
                for i in range(len(pieces)):
                    outer_diag(i).start()
        each_mask()
        for i in range(len(pieces)):
            outer_w(i).wait_send()
            outer_diag(i).wait_send()
        for j in range(per_half):
            e_far(j).wait_send()
            e_near(j).wait_send()

    @pl.when(jnp.logical_and(inner, near))
    def _():
        for i in range(len(pieces)):
            far_w(i).start()
        e_far(0).start()
        own_w().start()
        for j in range(per_half):
            own_e(j).start()
            near_e(j).start()
        for i in range(len(pieces)):
            for u in range(2):
                got_w(first + u, part, i)
                to_x(first + u, i).start()
                to_y(first + u, i).start()
                to_far(first + u, i).start()
        for j in range(1, per_half):
            e_far(j).start()
        each_mask()
        take_e(0)
        own_w().wait()
        for q in range(PARTS):
            at = pl.ds(q * quarter, quarter)
            beside = second + other
            arrived(wbuf.at[beside, at], w_recv.at[beside, q, 0])
        for i in range(len(pieces)):
            for u in range(2):
                for q in (x_part, y_part, d_part):
                    got_w(first + u, q, i)
        take_e(1)

        def turn(j):
            @pl.when(j > 1)
            def _():
                take_e(j)
            have_e(j)
            all_quarters(j)
            score(j)

        loop(per_half, turn)
        loop(per_half, finish)
        settle()
        for i in range(len(pieces)):
            for u in range(2):
                to_x(first + u, i).wait_send()
                to_y(first + u, i).wait_send()
                to_far(first + u, i).wait_send()

    @pl.when(jnp.logical_and(inner, jnp.logical_not(near)))
    def _():
        for i in range(len(pieces)):
            far_w(i).start()
        for j in range(per_half):
            e_far(j).start()
        for i in range(PARTS):
            near_w(i).start()
        for j in range(per_half):
            own_e(j).start()
            near_e(j).start()
        each_mask()
        for base in (first, second):
            for i in range(len(pieces)):
                for u in range(2):
                    got_w(base + u, part, i)
                    to_x(base + u, i).start()
                    to_y(base + u, i).start()

        def relays(base):
            for i in range(len(pieces)):
                for u in range(2):
                    for q in (x_part, y_part):
                        got_w(base + u, q, i)
                    relay(base + u, u, i).start()

        relays(first)
        take_e(0)
        take_e(1)

        def early(j):
            have_e(j)
            project(part, j)

        loop(2, early)
        relays(second)

        def middle(j):
            @pl.when(j == 2)
            def _():
                take_e(2)
                early(2)
            project(x_part, j)
            project(y_part, j)

        loop(3, middle)
        for i in range(len(pieces)):
            for u in range(2):
                for base in (first, second):
                    got_w(base + u, d_part, i)

        def late(j):
            project(d_part, j)
            score(j)

        loop(3, late)
        take_e(3)
        have_e(3)
        all_quarters(3)
        score(3)
        loop(per_half, finish)
        settle()
        for i in range(PARTS):
            near_w(i).wait_send()
        for i in range(len(pieces)):
            for base in (first, second):
                for u in range(2):
                    to_x(base + u, i).wait_send()
                    to_y(base + u, i).wait_send()
                    relay(base + u, u, i).wait_send()

    for h in range(2):
        local = jnp.logical_and(jnp.logical_and(inner, near), half == h)

        @pl.when(jnp.logical_not(local))
        def _():
            for j in range(per_half):
                arrived(rbuf.at[h * per_half + j], r_recv.at[h * per_half + j])

    for d in range(group - 1):
        mask_copy(d).wait_send()
        arrived(mbuf.at[others[d]], m_recv.at[others[d]])
    mbuf[me] = mine[...]
    counts = mbuf[0]
    for g in range(1, group):
        counts = counts + mbuf[g]
    counts = counts[:, :1].astype(jnp.float32)
    slot = lax.broadcasted_iota(jnp.int32, (prompts, rows), 1).astype(jnp.float32)
    cols = (slot < counts).astype(jnp.float32)
    pairs = jnp.maximum(counts - 1.0, 1.0)
    same = lax.broadcasted_iota(jnp.int32, (block_rows, block_rows), 0)
    same = (same == lax.broadcasted_iota(jnp.int32, (block_rows, block_rows), 1)).astype(jnp.float32)
    down = lax.dot_general(same, valid, NT, preferred_element_type=jnp.float32)
    lane = lax.broadcasted_iota(jnp.int32, (block_rows, 128), 1)
    rates = jnp.zeros((block_rows, 128), jnp.float32)
    for p in range(prompts):
        given = down[:, p:p + 1]
        prefs = jax.nn.sigmoid(rbuf[p].astype(jnp.float32)) * given * cols[p:p + 1, :]
        o_ref[p] = prefs
        totals = jnp.sum(prefs, axis=1, keepdims=True) - 0.5 * given
        rates = jnp.where(lane == p, given * totals / pairs[p:p + 1, :], rates)
    r_ref[...] = jnp.transpose(rates)[:prompts]


def line_scores(embeddings, head_weight, mask):
    prompts, block_rows, features = embeddings.shape
    held = head_weight.shape[0]
    group = CHIPS * CORES
    side = group // 2
    per_half = prompts // 2
    rows = group * block_rows
    half_rows = rows // 2
    quarter = held // PARTS
    bf16, f32 = jnp.bfloat16, jnp.float32
    dma = pltpu.SemaphoreType.DMA
    anywhere = pl.BlockSpec(memory_space=pl.ANY)
    vmem = pl.BlockSpec(memory_space=pltpu.VMEM)
    return pl.pallas_call(
        kernel,
        out_shape=(
            jax.ShapeDtypeStruct((prompts, block_rows, rows), f32),
            jax.ShapeDtypeStruct((prompts, block_rows), f32),
        ),
        in_specs=[anywhere, anywhere, vmem],
        out_specs=(vmem, vmem),
        scratch_shapes=[
            pltpu.VMEM((per_half, group, block_rows, features), bf16),
            pltpu.VMEM((side, held, features), bf16),
            pltpu.VMEM((per_half, side, held, rows), bf16),
            pltpu.VMEM((rows, rows), f32),
            pltpu.VMEM((per_half, half_rows, rows), f32),
            pltpu.VMEM((per_half, half_rows, rows), f32),
            pltpu.VMEM((per_half, half_rows, rows), f32),
            pltpu.VMEM((per_half, half_rows, rows), bf16),
            pltpu.VMEM((prompts, block_rows, rows), bf16),
            pltpu.VMEM((prompts, 128), jnp.int32),
            pltpu.VMEM((group, prompts, 128), jnp.int32),
            dma((group - 1,)),
            dma((group,)),
            dma((2, per_half)),
            dma((per_half, group)),
            dma((per_half,)),
            dma((per_half, 3)),
            dma((per_half,)),
            dma((4,)),
            dma((4,)),
            dma((4,)),
            dma((PARTS,)),
            dma((1,)),
            dma((side, 4)),
            dma((side, 4)),
            dma((side, 4)),
            dma((side, 4)),
            dma((side, PARTS, 4)),
            dma((per_half,)),
            dma((per_half,)),
            dma((per_half, side)),
            dma((prompts,)),
        ],
        compiler_params=pltpu.CompilerParams(
            collective_id=0, has_side_effects=True, vmem_limit_bytes=56 << 20
        ),
    )(embeddings, head_weight, mask)


def shards(embeddings, head_weight, valid_mask):
    group_size = lax.axis_size("resp")
    slots = group_size * embeddings.shape[1]
    if (lax.axis_size("prompt"), group_size) == (PARTS, CHIPS * CORES):
        return line_scores(embeddings, head_weight, valid_mask)
    valid_rows = valid_mask.astype(jnp.float32)
    counts = lax.psum(jnp.sum(valid_rows, axis=1), "resp")
    scores = gathered_scores(embeddings, head_weight)
    column_ids = jnp.arange(slots, dtype=jnp.float32)
    valid_cols = (column_ids[None, :] < counts[:, None]).astype(jnp.float32)
    preferences = jax.nn.sigmoid(scores) * valid_rows[:, :, None] * valid_cols[:, None, :]
    totals = jnp.sum(preferences, axis=2) - 0.5 * valid_rows
    win_rates = valid_rows * totals / jnp.maximum(counts - 1.0, 1.0)[:, None]
    return (preferences, win_rates)


def solution(mesh):
    return jax.shard_map(
        shards,
        mesh=mesh,
        in_specs=(P("prompt", "resp", None), P("resp", None), P("prompt", "resp")),
        out_specs=(P("prompt", "resp", None), P("prompt", "resp")),
        check_vma=False,
    )
```

time: 106 us -> 116 us (1.094)
  Pallas kernels: 102 us -> 112 us
    pallas_call x1, Pallas kernels: 102 us -> 112 us  [line_scores(): pl.pallas_call(kernel, out_shape=(jax.ShapeDtypeStruct((prompts, block_ro...]
where the time goes in v1:
time: 116 us
  Pallas kernels  112 us (97%)
  local copies, waits for them, and re-layouts  2.95 us (3%)
    pallas_call x1, Pallas kernels, line_scores(): pl.pallas_call(kernel, out_shape=(jax.ShapeDtypeStruct((prompts, block_ro...  112 us
    unnamed x2, local copies, waits for them, and re-layouts  2.95 us

profile of v1, /device:TPU:0, one launch (start us, length us, event | category | flops | bytes accessed | tf_op | source)
XLA Modules:
  0.0 115.9 jit_solution(4302213696194356623)
XLA Ops:
  0.6 112.4 %shard_map.50 = (f32[8,32,256]{2,1,0:T(8,128)}, f32[8,32]{1,0:T(8,128)}) custom-call(bf16[8,32,3584]{2,1,0:T(8,128)(2,1)} %e_ref.1, bf16[448,3584]{1,0:T(8,128)(2,1)} %w_ref.1, s32[8,32]{1,0:T(8,128)} %m_ref.1), custom_call_target="tpu_custom_call" | custom-call | tf_op jit(solution)/shard_map/pallas_call | solution.py:447
  113.0 1.7 %copy.7 = f32[8,32,256]{2,1,0:T(8,128)} copy(f32[8,32,256]{2,1,0:T(8,128)} %get-tuple-element.4) | data formatting | bytes 524288
  114.7 1.3 %copy.8 = f32[8,32]{1,0:T(8,128)} copy(f32[8,32]{1,0:T(8,128)} %get-tuple-element.5) | data formatting | bytes 2048

commit v2 on v1

--- a/solution.py
+++ b/solution.py
@@ -48,9 +48,9 @@
 
 
 def kernel(e_ref, w_ref, m_ref, o_ref, r_ref,
-           ebuf, wbuf, zt, sbuf, keep, pbuf, qbuf, fbuf, rbuf, mine, mbuf,
+           ebuf, wbuf, gbuf, zt, sbuf, keep, pbuf, qbuf, fbuf, rbuf, mine, mbuf,
            m_send, m_recv, e_send, e_recv, n_send, h_send, el_sem,
-           o_send, d_send, f_send, nw_send, wl_sem, x_send, y_send, u_send, v_send, w_recv,
+           o_send, d_send, nw_send, wl_sem, g_recv, x_send, y_send, u_send, v_send, w_recv,
            p_send, p_recv, r_send, r_recv):
     part = lax.axis_index("prompt")
     me = lax.axis_index("resp")
@@ -79,6 +79,7 @@
     x_part = part + 1 - 2 * (part % 2)
     y_part = lax.rem(part + 2, PARTS)
     d_part = PARTS - 1 - part
+    chip_width = features // CHIPS
     step = quarter // 7
     pieces = ((0, step), (step, 2 * step), (3 * step, 2 * step), (5 * step, 2 * step))
 
@@ -93,6 +94,10 @@
 
     valid = m_ref[...].astype(jnp.float32)
     mine[...] = jnp.broadcast_to(jnp.sum(m_ref[...], axis=1, keepdims=True), mine.shape)
+
+    folded = pl.ds(jnp.where(near, second, first), 2)
+    away_cols = pl.ds(pl.multiple_of(jnp.where(near, z_out, 3 - z_out) * chip_width, 128), chip_width)
+    wbuf[folded, :, away_cols] = jnp.zeros((2, held, chip_width), jnp.bfloat16)
 
     others = [lax.rem(me + d, group) for d in range(1, group)]
     barrier = pltpu.get_barrier_semaphore()
@@ -108,13 +113,21 @@
             device_id=(part, others[d]), device_id_type=MESH,
         )
 
-    def w_rows(block, q, i):
+    def chip_cols(chip):
+        return pl.ds(pl.multiple_of(chip * chip_width, 128), chip_width)
+
+    def kept_cols(h):
+        return pl.ds(pl.multiple_of((1 - h) * chip_width, 128), features - chip_width)
+
+    every = pl.ds(0, features)
+
+    def w_rows(block, q, i, cols=every):
         at, size = pieces[i]
-        return wbuf.at[block, pl.ds(pl.multiple_of(q * quarter + at, 16), size)]
-
-    def my_rows(q, i):
+        return wbuf.at[block, pl.ds(pl.multiple_of(q * quarter + at, 16), size), cols]
+
+    def my_rows(q, i, cols=every):
         at, size = pieces[i]
-        return w_ref.at[pl.ds(pl.multiple_of(q * quarter + at, 16), size)]
+        return w_ref.at[pl.ds(pl.multiple_of(q * quarter + at, 16), size), cols]
 
     def outer_w(i):
         return copy(my_rows(part, i), w_rows(here, part, i), o_send.at[i], w_recv.at[here, part, i], z_in, half)
@@ -123,42 +136,58 @@
         return copy(my_rows(d_part, i), w_rows(here, d_part, i), d_send.at[i], w_recv.at[here, d_part, i], z_in, half)
 
     def far_w(i):
-        return copy(my_rows(part, i), w_rows(here, part, i), o_send.at[i], w_recv.at[here, part, i], z_far, half)
+        cols = kept_cols(half)
+        return copy(my_rows(part, i, cols), w_rows(here, part, i, cols), o_send.at[i],
+                    w_recv.at[here, part, i], z_far, half)
 
     def near_w(i):
         at = pl.ds(i * quarter, quarter)
-        return copy(w_ref.at[at], wbuf.at[here, at], nw_send.at[i], w_recv.at[here, i, 0], z_in, half)
+        cols = kept_cols(half)
+        return copy(w_ref.at[at, cols], wbuf.at[here, at, cols], nw_send.at[i], w_recv.at[here, i, 0], z_in, half)
+
+    def near_g():
+        return copy(w_ref.at[:, chip_cols(z_out)], gbuf.at[core], nw_send.at[PARTS], g_recv.at[0], z_in, half)
 
     def own_w():
-        return pltpu.make_async_copy(w_ref, wbuf.at[here], wl_sem.at[0])
-
-    def got_w(block, q, i):
-        arrived(w_rows(block, q, i), w_recv.at[block, q, i])
-
-    def along(block, q, i, sems, chip, q_to):
-        spot = w_rows(block, q, i)
+        cols = kept_cols(half)
+        return pltpu.make_async_copy(w_ref.at[:, cols], wbuf.at[here, :, cols], wl_sem.at[0])
+
+    def own_g():
+        return pltpu.make_async_copy(w_ref.at[:, chip_cols(z_out)], gbuf.at[core], wl_sem.at[1])
+
+    def fold(q, at, size):
+        start = q * quarter + at
+        row = lax.broadcasted_iota(jnp.int32, (2 * size, chip_width), 0)
+        col = lax.broadcasted_iota(jnp.int32, (2 * size, chip_width), 1)
+        pick = (start + jnp.where(row < size, row, row + held - size) == col).astype(jnp.bfloat16)
+        turned = lax.dot_general(
+            pick, gbuf[...].reshape(chip_width, chip_width), NT, preferred_element_type=jnp.float32
+        ).reshape(2, size, chip_width)
+        pair, where, cols = pl.ds(first, 2), pl.ds(pl.multiple_of(start, 16), size), chip_cols(z_in)
+        wbuf[pair, where, cols] = (wbuf[pair, where, cols].astype(jnp.float32) - turned).astype(jnp.bfloat16)
+
+    def got_w(block, q, i, cols=every):
+        arrived(w_rows(block, q, i, cols), w_recv.at[block, q, i])
+
+    def along(block, q, i, sems, chip, q_to, cols):
+        spot = w_rows(block, q, i, cols)
         return copy(spot, spot, sems.at[block, i], w_recv.at[block, q, i], chip, core, q_to)
 
-    def to_x(block, i):
-        return along(block, part, i, x_send, z_in, x_part)
-
-    def to_y(block, i):
-        return along(block, part, i, y_send, z_in, y_part)
+    def to_x(block, i, cols=every):
+        return along(block, part, i, x_send, z_in, x_part, cols)
+
+    def to_y(block, i, cols=every):
+        return along(block, part, i, y_send, z_in, y_part, cols)
 
     def to_far(block, i):
-        return along(block, part, i, u_send, z_far, part)
-
-    def x_to_y(block, i):
-        return along(block, x_part, i, v_send, z_in, y_part)
-
-    def y_to_x(block, i):
-        return along(block, y_part, i, v_send, z_in, x_part)
-
-    def relay(block, u, i):
-        return x_to_y(block, i) if (i < 2) == (u == 0) else y_to_x(block, i)
-
-    def e_copy(h, j):
-        return copy(e_ref.at[h * per_half + j], ebuf.at[j, me], e_send.at[h, j], e_recv.at[j, me], 1 + h, core)
+        return along(block, part, i, u_send, z_far, part, every)
+
+    def relay(block, u, i, cols=every):
+        if (i < 2) == (u == 0):
+            return along(block, x_part, i, v_send, z_in, y_part, cols)
+        return along(block, y_part, i, v_send, z_in, x_part, cols)
+
+    passed = ((first, kept_cols(1 - half)), (second, every))
 
     def e_far(j):
         return copy(e_ref.at[(1 - half) * per_half + j], ebuf.at[j, me], e_send.at[1, j], e_recv.at[j, me], z_far, core)
@@ -266,148 +295,127 @@
     def _():
         for i in range(len(pieces)):
             outer_w(i).start()
+        each_mask()
+        for i in range(len(pieces)):
+            outer_diag(i).start()
         for j in range(per_half):
             e_far(j).start()
             e_near(j).start()
-            if j == 0:
-                for i in range(len(pieces)):
-                    outer_diag(i).start()
+
+    @pl.when(jnp.logical_and(inner, near))
+    def _():
+        for i in range(len(pieces)):
+            far_w(i).start()
         each_mask()
-        for i in range(len(pieces)):
-            outer_w(i).wait_send()
-            outer_diag(i).wait_send()
-        for j in range(per_half):
-            e_far(j).wait_send()
-            e_near(j).wait_send()
-
-    @pl.when(jnp.logical_and(inner, near))
-    def _():
-        for i in range(len(pieces)):
-            far_w(i).start()
-        e_far(0).start()
+        own_g().start()
         own_w().start()
         for j in range(per_half):
             own_e(j).start()
             near_e(j).start()
+        own_g().wait()
+        arrived(gbuf.at[other], g_recv.at[0])
         for i in range(len(pieces)):
             for u in range(2):
                 got_w(first + u, part, i)
+            fold(part, *pieces[i])
+            for u in range(2):
+                to_far(first + u, i).start()
                 to_x(first + u, i).start()
                 to_y(first + u, i).start()
-                to_far(first + u, i).start()
-        for j in range(1, per_half):
+        for j in range(per_half):
             e_far(j).start()
-        each_mask()
-        take_e(0)
         own_w().wait()
         for q in range(PARTS):
             at = pl.ds(q * quarter, quarter)
             beside = second + other
-            arrived(wbuf.at[beside, at], w_recv.at[beside, q, 0])
+            arrived(wbuf.at[beside, at, kept_cols(half)], w_recv.at[beside, q, 0])
         for i in range(len(pieces)):
             for u in range(2):
                 for q in (x_part, y_part, d_part):
                     got_w(first + u, q, i)
-        take_e(1)
+        fold(d_part, 0, quarter)
 
         def turn(j):
-            @pl.when(j > 1)
-            def _():
-                take_e(j)
+            take_e(j)
             have_e(j)
             all_quarters(j)
+
+            @pl.when(j == per_half - 1)
+            def _():
+                loop(per_half - 1, finish)
             score(j)
 
         loop(per_half, turn)
-        loop(per_half, finish)
-        settle()
-        for i in range(len(pieces)):
-            for u in range(2):
-                to_x(first + u, i).wait_send()
-                to_y(first + u, i).wait_send()
-                to_far(first + u, i).wait_send()
+        finish(per_half - 1)
 
     @pl.when(jnp.logical_and(inner, jnp.logical_not(near)))
     def _():
+        near_g().start()
         for i in range(len(pieces)):
             far_w(i).start()
-        for j in range(per_half):
-            e_far(j).start()
+        each_mask()
         for i in range(PARTS):
             near_w(i).start()
         for j in range(per_half):
             own_e(j).start()
             near_e(j).start()
-        each_mask()
-        for base in (first, second):
+        for base, cols in passed:
             for i in range(len(pieces)):
                 for u in range(2):
-                    got_w(base + u, part, i)
-                    to_x(base + u, i).start()
-                    to_y(base + u, i).start()
-
-        def relays(base):
+                    got_w(base + u, part, i, cols)
+                    to_x(base + u, i, cols).start()
+                    to_y(base + u, i, cols).start()
+        for j in range(per_half):
+            e_far(j).start()
+
+        def relays(base, cols, i):
+            for u in range(2):
+                for q in (x_part, y_part):
+                    got_w(base + u, q, i, cols)
+                relay(base + u, u, i, cols).start()
+
+        for i in range(len(pieces)):
+            relays(*passed[0], i)
+        take_e(0)
+        have_e(0)
+        project(part, 0)
+        for i in range(len(pieces)):
+            if i == len(pieces) - 1:
+                take_e(1)
+            relays(*passed[1], i)
+
+        def middle(j):
+            @pl.when(j > 0)
+            def _():
+                @pl.when(j > 1)
+                def _():
+                    take_e(j)
+                have_e(j)
+                project(part, j)
+            project(x_part, j)
+            project(y_part, j)
+
+        loop(3, middle)
+        for base, cols in passed:
             for i in range(len(pieces)):
                 for u in range(2):
-                    for q in (x_part, y_part):
-                        got_w(base + u, q, i)
-                    relay(base + u, u, i).start()
-
-        relays(first)
-        take_e(0)
-        take_e(1)
-
-        def early(j):
-            have_e(j)
-            project(part, j)
-
-        loop(2, early)
-        relays(second)
-
-        def middle(j):
+                    got_w(base + u, d_part, i, cols)
+
+        def late(j):
             @pl.when(j == 2)
             def _():
-                take_e(2)
-                early(2)
-            project(x_part, j)
-            project(y_part, j)
-
-        loop(3, middle)
-        for i in range(len(pieces)):
-            for u in range(2):
-                for base in (first, second):
-                    got_w(base + u, d_part, i)
-
-        def late(j):
+                take_e(3)
             project(d_part, j)
             score(j)
 
         loop(3, late)
-        take_e(3)
+        loop(3, finish)
         have_e(3)
         all_quarters(3)
         score(3)
-        loop(per_half, finish)
-        settle()
-        for i in range(PARTS):
-            near_w(i).wait_send()
-        for i in range(len(pieces)):
-            for base in (first, second):
-                for u in range(2):
-                    to_x(base + u, i).wait_send()
-                    to_y(base + u, i).wait_send()
-                    relay(base + u, u, i).wait_send()
-
-    for h in range(2):
-        local = jnp.logical_and(jnp.logical_and(inner, near), half == h)
-
-        @pl.when(jnp.logical_not(local))
-        def _():
-            for j in range(per_half):
-                arrived(rbuf.at[h * per_half + j], r_recv.at[h * per_half + j])
+        finish(3)
 
     for d in range(group - 1):
-        mask_copy(d).wait_send()
         arrived(mbuf.at[others[d]], m_recv.at[others[d]])
     mbuf[me] = mine[...]
     counts = mbuf[0]
@@ -422,13 +430,55 @@
     down = lax.dot_general(same, valid, NT, preferred_element_type=jnp.float32)
     lane = lax.broadcasted_iota(jnp.int32, (block_rows, 128), 1)
     rates = jnp.zeros((block_rows, 128), jnp.float32)
-    for p in range(prompts):
-        given = down[:, p:p + 1]
-        prefs = jax.nn.sigmoid(rbuf[p].astype(jnp.float32)) * given * cols[p:p + 1, :]
-        o_ref[p] = prefs
-        totals = jnp.sum(prefs, axis=1, keepdims=True) - 0.5 * given
-        rates = jnp.where(lane == p, given * totals / pairs[p:p + 1, :], rates)
+    for j in range(per_half):
+        for h in range(2):
+            p = h * per_half + j
+
+            @pl.when(jnp.logical_not(jnp.logical_and(jnp.logical_and(inner, near), half == h)))
+            def _():
+                arrived(rbuf.at[p], r_recv.at[p])
+            given = down[:, p:p + 1]
+            prefs = jax.nn.sigmoid(rbuf[p].astype(jnp.float32)) * given * cols[p:p + 1, :]
+            o_ref[p] = prefs
+            totals = jnp.sum(prefs, axis=1, keepdims=True) - 0.5 * given
+            rates = jnp.where(lane == p, given * totals / pairs[p:p + 1, :], rates)
     r_ref[...] = jnp.transpose(rates)[:prompts]
+
+    for d in range(group - 1):
+        mask_copy(d).wait_send()
+
+    @pl.when(jnp.logical_not(inner))
+    def _():
+        for i in range(len(pieces)):
+            outer_w(i).wait_send()
+            outer_diag(i).wait_send()
+        for j in range(per_half):
+            e_far(j).wait_send()
+            e_near(j).wait_send()
+
+    @pl.when(inner)
+    def _():
+        settle()
+
+    @pl.when(jnp.logical_and(inner, near))
+    def _():
+        for i in range(len(pieces)):
+            for u in range(2):
+                to_x(first + u, i).wait_send()
+                to_y(first + u, i).wait_send()
+                to_far(first + u, i).wait_send()
+
+    @pl.when(jnp.logical_and(inner, jnp.logical_not(near)))
+    def _():
+        near_g().wait_send()
+        for i in range(PARTS):
+            near_w(i).wait_send()
+        for i in range(len(pieces)):
+            for base, cols in passed:
+                for u in range(2):
+                    to_x(base + u, i, cols).wait_send()
+                    to_y(base + u, i, cols).wait_send()
+                    relay(base + u, u, i, cols).wait_send()
 
 
 def line_scores(embeddings, head_weight, mask):
@@ -455,6 +505,7 @@
         scratch_shapes=[
             pltpu.VMEM((per_half, group, block_rows, features), bf16),
             pltpu.VMEM((side, held, features), bf16),
+            pltpu.VMEM((CORES, held, features // CHIPS), bf16),
             pltpu.VMEM((per_half, side, held, rows), bf16),
             pltpu.VMEM((rows, rows), f32),
             pltpu.VMEM((per_half, half_rows, rows), f32),
@@ -473,8 +524,8 @@
             dma((per_half,)),
             dma((4,)),
             dma((4,)),
-            dma((4,)),
-            dma((PARTS,)),
+            dma((PARTS + 1,)),
+            dma((2,)),
             dma((1,)),
             dma((side, 4)),
             dma((side, 4)),

time: 116 us -> 100 us (0.86)
  Pallas kernels: 112 us -> 96.6 us
    pallas_call x1, Pallas kernels: 112 us -> 96.6 us  [line_scores(): pl.pallas_call(kernel, out_shape=(jax.ShapeDtypeStruct((prompts, block_ro...]
where the time goes in v2:
time: 100 us
  Pallas kernels  96.6 us (97%)
  local copies, waits for them, and re-layouts  2.95 us (3%)
    pallas_call x1, Pallas kernels, line_scores(): pl.pallas_call(kernel, out_shape=(jax.ShapeDtypeStruct((prompts, block_ro...  96.6 us
    unnamed x2, local copies, waits for them, and re-layouts  2.95 us

profile of v2, /device:TPU:0, one launch (start us, length us, event | category | flops | bytes accessed | tf_op | source)
XLA Modules:
  0.0 100.2 jit_solution(8882245925784111606)
XLA Ops:
  0.6 96.6 %shard_map.50 = (f32[8,32,256]{2,1,0:T(8,128)}, f32[8,32]{1,0:T(8,128)}) custom-call(bf16[8,32,3584]{2,1,0:T(8,128)(2,1)} %e_ref.1, bf16[448,3584]{1,0:T(8,128)(2,1)} %w_ref.1, s32[8,32]{1,0:T(8,128)} %m_ref.1), custom_call_target="tpu_custom_call" | custom-call | tf_op jit(solution)/shard_map/pallas_call | solution.py:497
  97.2 1.7 %copy.7 = f32[8,32,256]{2,1,0:T(8,128)} copy(f32[8,32,256]{2,1,0:T(8,128)} %get-tuple-element.4) | data formatting | bytes 524288
  98.9 1.3 %copy.8 = f32[8,32]{1,0:T(8,128)} copy(f32[8,32]{1,0:T(8,128)} %get-tuple-element.5) | data formatting | bytes 2048

commit v3 on v2

--- a/solution.py
+++ b/solution.py
@@ -11,6 +11,8 @@
 CORES = 2
 CHIPS = 4
 PARTS = 4
+CHUNKS = 2
+DIRECT = 3
 NT = (((1,), (1,)), ((), ()))
 
 
@@ -47,9 +49,9 @@
     return lax.map(scores_of, pieces).reshape(prompts, block_rows, slots)
 
 
-def kernel(e_ref, w_ref, m_ref, o_ref, r_ref,
-           ebuf, wbuf, gbuf, zt, sbuf, keep, pbuf, qbuf, fbuf, rbuf, mine, mbuf,
-           m_send, m_recv, e_send, e_recv, n_send, h_send, el_sem,
+def kernel(e_ref, w_ref, m_hbm, o_ref, r_ref,
+           m_ref, ebuf, wbuf, gbuf, zt, zsum, sbuf, keep, pbuf, qbuf, fbuf, rbuf, mine, mbuf,
+           m_sem, m_send, m_recv, e_send, e_recv, n_send, h_send, el_sem,
            o_send, d_send, nw_send, wl_sem, g_recv, x_send, y_send, u_send, v_send, w_recv,
            p_send, p_recv, r_send, r_recv):
     part = lax.axis_index("prompt")
@@ -81,7 +83,10 @@
     d_part = PARTS - 1 - part
     chip_width = features // CHIPS
     step = quarter // 7
+    last = per_half - 1
     pieces = ((0, step), (step, 2 * step), (3 * step, 2 * step), (5 * step, 2 * step))
+
+    chunk_width = features // CHUNKS
 
     def copy(src, dst, send, recv, chip, c, q=None):
         return pltpu.make_async_remote_copy(
@@ -92,20 +97,14 @@
     def arrived(dst, recv):
         copy(dst, dst, m_send.at[0], recv, z_far, core).wait_recv()
 
-    valid = m_ref[...].astype(jnp.float32)
-    mine[...] = jnp.broadcast_to(jnp.sum(m_ref[...], axis=1, keepdims=True), mine.shape)
-
-    folded = pl.ds(jnp.where(near, second, first), 2)
-    away_cols = pl.ds(pl.multiple_of(jnp.where(near, z_out, 3 - z_out) * chip_width, 128), chip_width)
-    wbuf[folded, :, away_cols] = jnp.zeros((2, held, chip_width), jnp.bfloat16)
-
+    m_copy = pltpu.make_async_copy(m_hbm, m_ref, m_sem.at[0])
+    m_copy.start()
     others = [lax.rem(me + d, group) for d in range(1, group)]
     barrier = pltpu.get_barrier_semaphore()
     for peer in others:
         pl.semaphore_signal(barrier, inc=1, device_id=(part, peer), device_id_type=MESH)
     for q in (x_part, y_part):
         pl.semaphore_signal(barrier, inc=1, device_id=(q, me), device_id_type=MESH)
-    pl.semaphore_wait(barrier, len(others) + 2)
 
     def mask_copy(d):
         return pltpu.make_async_remote_copy(
@@ -189,47 +188,88 @@
 
     passed = ((first, kept_cols(1 - half)), (second, every))
 
-    def e_far(j):
-        return copy(e_ref.at[(1 - half) * per_half + j], ebuf.at[j, me], e_send.at[1, j], e_recv.at[j, me], z_far, core)
-
-    def e_near(j):
-        return copy(e_ref.at[half * per_half + j], ebuf.at[j, me], e_send.at[0, j], e_recv.at[j, me], z_in, core)
+    def chunk_cols(k):
+        return pl.ds(pl.multiple_of(k * chunk_width, 128), chunk_width)
+
+    def e_part(j, block, k):
+        if k is None:
+            return ebuf.at[j, block]
+        return ebuf.at[j, block, :, chunk_cols(k)]
+
+    def e_mine(h, j, k):
+        if k is None:
+            return e_ref.at[h * per_half + j]
+        return e_ref.at[h * per_half + j, :, chunk_cols(k)]
+
+    def e_far(j, k=None):
+        unit = j if k is None else j + k
+        return copy(e_mine(1 - half, j, k), e_part(j, me, k), e_send.at[1, unit], e_recv.at[unit, me], z_far, core)
+
+    def e_near(j, k=None):
+        unit = j if k is None else j + k
+        return copy(e_mine(half, j, k), e_part(j, me, k), e_send.at[0, unit], e_recv.at[unit, me], z_in, core)
 
     def near_e(j):
-        return copy(e_ref.at[half * per_half + j], ebuf.at[j, me], n_send.at[j], e_recv.at[j, me], z_in, other)
+        return copy(e_mine(half, j, None), ebuf.at[j, me], n_send.at[j], e_recv.at[j, me], z_in, other)
 
     def own_e(j):
-        return pltpu.make_async_copy(e_ref.at[half * per_half + j], ebuf.at[j, me], el_sem.at[j])
+        return pltpu.make_async_copy(e_mine(half, j, None), ebuf.at[j, me], el_sem.at[j])
 
     away = (z_out, z_far, z_end)
 
-    def pass_e(j, k):
-        block = away[k] * CORES + core
-        spot = ebuf.at[j, block]
-        return copy(spot, spot, h_send.at[j, k], e_recv.at[j, block], z_in, other)
-
-    def take_e(j):
-        for k in range(3):
-            block = away[k] * CORES + core
-            arrived(ebuf.at[j, block], e_recv.at[j, block])
-            pass_e(j, k).start()
-
-    def have_e(j):
+    def pass_e(j, n, k=None):
+        unit = j if k is None else j + k
+        block = away[n] * CORES + core
+        spot = e_part(j, block, k)
+        return copy(spot, spot, h_send.at[unit, n], e_recv.at[unit, block], z_in, other)
+
+    def take_e(j, k=None):
+        unit = j if k is None else j + k
+        for n in range(3):
+            block = away[n] * CORES + core
+            arrived(e_part(j, block, k), e_recv.at[unit, block])
+            pass_e(j, n, k).start()
+
+    def have_own(j):
         own_e(j).wait()
-        for chip in (z_in,) + away:
+        beside = z_in * CORES + other
+        arrived(ebuf.at[j, beside], e_recv.at[j, beside])
+
+    def have_e(j, k=None):
+        unit = j if k is None else j + k
+        for chip in away:
             block = chip * CORES + other
-            arrived(ebuf.at[j, block], e_recv.at[j, block])
+            arrived(e_part(j, block, k), e_recv.at[unit, block])
+
+    def all_units(act):
+        for j in range(last):
+            act(j, None)
+        for k in range(CHUNKS):
+            act(last, k)
 
     def partial_copy(j):
         return copy(pbuf.at[j], qbuf.at[j], p_send.at[j], p_recv.at[j], z_in, other)
 
-    def project(q, j):
+    def project(q, j, base, many):
         at = pl.ds(pl.multiple_of(q * quarter, 16), quarter)
-        left = wbuf[:, at].reshape(side * quarter, features)
+        blocks = pl.ds(base, many)
+        left = wbuf[blocks, at].reshape(many * quarter, features)
         right = ebuf[j].reshape(rows, features)
-        zt[j, :, at] = lax.dot_general(
+        zt[j, blocks, at] = lax.dot_general(
             left, right, NT, preferred_element_type=jnp.float32
-        ).astype(jnp.bfloat16).reshape(side, quarter, rows)
+        ).astype(jnp.bfloat16).reshape(many, quarter, rows)
+
+    def project_last(k):
+        cols = chunk_cols(k)
+        left = wbuf[:, :, cols].reshape(side * held, chunk_width)
+        right = ebuf[last, :, :, cols].reshape(rows, chunk_width)
+        total = lax.dot_general(
+            left, right, NT, preferred_element_type=jnp.float32
+        ).reshape(side, held, rows)
+        zsum[...] = jnp.where(k > 0, zsum[...], 0.0) + total
+
+    def settle_last():
+        zt[last] = zsum[...].astype(jnp.bfloat16)
 
     lanes = pl.ds(pl.multiple_of(core * span, 128), span)
     mine_at = pl.multiple_of(core * half_rows, half_rows)
@@ -272,11 +312,14 @@
             mask_copy(d).start()
 
     def settle():
+        def sent(j, k):
+            e_far(j, k).wait_send()
+            for n in range(3):
+                pass_e(j, n, k).wait_send()
+
+        all_units(sent)
         for j in range(per_half):
-            e_far(j).wait_send()
             near_e(j).wait_send()
-            for k in range(3):
-                pass_e(j, k).wait_send()
             partial_copy(j).wait_send()
             each_target(j, lambda c: c.wait_send())
         for i in range(len(pieces)):
@@ -288,29 +331,55 @@
             return carry
         lax.fori_loop(0, n, run, 0)
 
-    def all_quarters(j):
-        loop(PARTS, lambda q: project(q, j))
+    def choose(index, values):
+        picked = values[0]
+        for n in range(1, len(values)):
+            picked = jnp.where(index == n, values[n], picked)
+        return picked
+
+    @pl.when(inner)
+    def _():
+        @pl.when(near)
+        def _():
+            own_g().start()
+            own_w().start()
+        for j in range(per_half):
+            own_e(j).start()
+
+    folded = pl.ds(jnp.where(near, second, first), 2)
+    away_cols = pl.ds(pl.multiple_of(jnp.where(near, z_out, 3 - z_out) * chip_width, 128), chip_width)
+    wbuf[folded, :, away_cols] = jnp.zeros((2, held, chip_width), jnp.bfloat16)
+    m_copy.wait()
+    valid = m_ref[...].astype(jnp.float32)
+    mine[...] = jnp.broadcast_to(jnp.sum(m_ref[...], axis=1, keepdims=True), mine.shape)
+    pl.semaphore_wait(barrier, len(others) + 2)
 
     @pl.when(jnp.logical_not(inner))
     def _():
         for i in range(len(pieces)):
             outer_w(i).start()
         each_mask()
-        for i in range(len(pieces)):
+        for i in range(DIRECT):
             outer_diag(i).start()
-        for j in range(per_half):
-            e_far(j).start()
-            e_near(j).start()
+
+        def send(j, k):
+            e_near(j, k).start()
+            e_far(j, k).start()
+
+        all_units(send)
+
+    def relays(base, cols, i):
+        for u in range(2):
+            for q in (x_part, y_part):
+                got_w(base + u, q, i, cols)
+            relay(base + u, u, i, cols).start()
 
     @pl.when(jnp.logical_and(inner, near))
     def _():
         for i in range(len(pieces)):
             far_w(i).start()
         each_mask()
-        own_g().start()
-        own_w().start()
         for j in range(per_half):
-            own_e(j).start()
             near_e(j).start()
         own_g().wait()
         arrived(gbuf.at[other], g_recv.at[0])
@@ -322,31 +391,64 @@
                 to_far(first + u, i).start()
                 to_x(first + u, i).start()
                 to_y(first + u, i).start()
-        for j in range(per_half):
-            e_far(j).start()
+        all_units(lambda j, k: e_far(j, k).start())
         own_w().wait()
         for q in range(PARTS):
             at = pl.ds(q * quarter, quarter)
             beside = second + other
             arrived(wbuf.at[beside, at, kept_cols(half)], w_recv.at[beside, q, 0])
         for i in range(len(pieces)):
+            if i >= DIRECT:
+                relays(first, every, i)
             for u in range(2):
-                for q in (x_part, y_part, d_part):
-                    got_w(first + u, q, i)
-        fold(d_part, 0, quarter)
-
-        def turn(j):
-            take_e(j)
-            have_e(j)
-            all_quarters(j)
-
-            @pl.when(j == per_half - 1)
-            def _():
-                loop(per_half - 1, finish)
-            score(j)
-
-        loop(per_half, turn)
-        finish(per_half - 1)
+                if i < DIRECT:
+                    got_w(first + u, x_part, i)
+                    got_w(first + u, y_part, i)
+
+        def turn(t):
+            j = t // PARTS
+            s = t % PARTS
+
+            @pl.when(s == 0)
+            def _():
+                take_e(j)
+                have_own(j)
+                have_e(j)
+
+            @pl.when(t == PARTS - 1)
+            def _():
+                for i in range(len(pieces)):
+                    for u in range(2):
+                        got_w(first + u, d_part, i)
+                fold(d_part, 0, pieces[DIRECT][0])
+
+            @pl.when(t == last * PARTS - 1)
+            def _():
+                take_e(last, 0)
+            project(choose(s, (part, x_part, y_part, d_part)), j, 0, side)
+
+            @pl.when(s == PARTS - 1)
+            def _():
+                score(j)
+
+        loop(last * PARTS, turn)
+        have_own(last)
+
+        def final_turn(k):
+            @pl.when(k < CHUNKS - 1)
+            def _():
+                take_e(last, k + 1)
+
+            @pl.when(k == CHUNKS - 1)
+            def _():
+                loop(last, finish)
+            have_e(last, k)
+            project_last(k)
+
+        loop(CHUNKS, final_turn)
+        settle_last()
+        score(last)
+        finish(last)
 
     @pl.when(jnp.logical_and(inner, jnp.logical_not(near)))
     def _():
@@ -357,7 +459,6 @@
         for i in range(PARTS):
             near_w(i).start()
         for j in range(per_half):
-            own_e(j).start()
             near_e(j).start()
         for base, cols in passed:
             for i in range(len(pieces)):
@@ -365,55 +466,66 @@
                     got_w(base + u, part, i, cols)
                     to_x(base + u, i, cols).start()
                     to_y(base + u, i, cols).start()
-        for j in range(per_half):
-            e_far(j).start()
-
-        def relays(base, cols, i):
-            for u in range(2):
-                for q in (x_part, y_part):
-                    got_w(base + u, q, i, cols)
-                relay(base + u, u, i, cols).start()
-
-        for i in range(len(pieces)):
-            relays(*passed[0], i)
-        take_e(0)
-        have_e(0)
-        project(part, 0)
-        for i in range(len(pieces)):
-            if i == len(pieces) - 1:
-                take_e(1)
-            relays(*passed[1], i)
-
-        def middle(j):
-            @pl.when(j > 0)
-            def _():
-                @pl.when(j > 1)
-                def _():
-                    take_e(j)
-                have_e(j)
-                project(part, j)
-            project(x_part, j)
-            project(y_part, j)
-
-        loop(3, middle)
-        for base, cols in passed:
+        all_units(lambda j, k: e_far(j, k).start())
+
+        def got_diag(base, cols):
             for i in range(len(pieces)):
                 for u in range(2):
                     got_w(base + u, d_part, i, cols)
 
-        def late(j):
-            @pl.when(j == 2)
-            def _():
-                take_e(3)
-            project(d_part, j)
-            score(j)
-
-        loop(3, late)
-        loop(3, finish)
-        have_e(3)
-        all_quarters(3)
-        score(3)
-        finish(3)
+        for i in range(len(pieces)):
+            relays(*passed[0], i)
+        take_e(0)
+        have_own(0)
+        have_e(0)
+        order = ((0, 0), (1, 0), (2, 0), (0, 1), (1, 1), (2, 1), (0, 2), (1, 2), (2, 2), (3, 0), (3, 1), (3, 2))
+
+        def turn(t):
+            what = choose(t, [q * PARTS + j for q, j in order])
+            j = what % PARTS
+
+            @pl.when(t == 1)
+            def _():
+                for i in range(len(pieces)):
+                    if i == len(pieces) - 1:
+                        take_e(1)
+                    relays(*passed[1], i)
+
+            @pl.when(t == 3)
+            def _():
+                have_own(1)
+                have_e(1)
+
+            @pl.when(t == 6)
+            def _():
+                take_e(2)
+                have_own(2)
+                have_e(2)
+
+            @pl.when(t == 9)
+            def _():
+                take_e(last, 0)
+                for base, cols in passed:
+                    got_diag(base, cols)
+            project(choose(what // PARTS, (part, x_part, y_part, d_part)), j, 0, side)
+
+        loop(len(order), turn)
+        have_own(last)
+        have_e(last, 0)
+        loop(last, score)
+        take_e(last, 1)
+        loop(last, finish)
+
+        def final_turn(k):
+            @pl.when(k > 0)
+            def _():
+                have_e(last, k)
+            project_last(k)
+
+        loop(CHUNKS, final_turn)
+        settle_last()
+        score(last)
+        finish(last)
 
     for d in range(group - 1):
         arrived(mbuf.at[others[d]], m_recv.at[others[d]])
@@ -430,18 +542,20 @@
     down = lax.dot_general(same, valid, NT, preferred_element_type=jnp.float32)
     lane = lax.broadcasted_iota(jnp.int32, (block_rows, 128), 1)
     rates = jnp.zeros((block_rows, 128), jnp.float32)
-    for j in range(per_half):
-        for h in range(2):
-            p = h * per_half + j
-
-            @pl.when(jnp.logical_not(jnp.logical_and(jnp.logical_and(inner, near), half == h)))
-            def _():
-                arrived(rbuf.at[p], r_recv.at[p])
-            given = down[:, p:p + 1]
-            prefs = jax.nn.sigmoid(rbuf[p].astype(jnp.float32)) * given * cols[p:p + 1, :]
-            o_ref[p] = prefs
-            totals = jnp.sum(prefs, axis=1, keepdims=True) - 0.5 * given
-            rates = jnp.where(lane == p, given * totals / pairs[p:p + 1, :], rates)
+    for batch in (range(last), range(last, per_half)):
+        for j in batch:
+            for h in range(2):
+                @pl.when(jnp.logical_not(jnp.logical_and(jnp.logical_and(inner, near), half == h)))
+                def _():
+                    arrived(rbuf.at[h * per_half + j], r_recv.at[h * per_half + j])
+        for j in batch:
+            for h in range(2):
+                p = h * per_half + j
+                given = down[:, p:p + 1]
+                prefs = jax.nn.sigmoid(rbuf[p].astype(jnp.float32)) * given * cols[p:p + 1, :]
+                o_ref[p] = prefs
+                totals = jnp.sum(prefs, axis=1, keepdims=True) - 0.5 * given
+                rates = jnp.where(lane == p, given * totals / pairs[p:p + 1, :], rates)
     r_ref[...] = jnp.transpose(rates)[:prompts]
 
     for d in range(group - 1):
@@ -451,10 +565,14 @@
     def _():
         for i in range(len(pieces)):
             outer_w(i).wait_send()
+        for i in range(DIRECT):
             outer_diag(i).wait_send()
-        for j in range(per_half):
-            e_far(j).wait_send()
-            e_near(j).wait_send()
+
+        def left(j, k):
+            e_far(j, k).wait_send()
+            e_near(j, k).wait_send()
+
+        all_units(left)
 
     @pl.when(inner)
     def _():
@@ -467,6 +585,8 @@
                 to_x(first + u, i).wait_send()
                 to_y(first + u, i).wait_send()
                 to_far(first + u, i).wait_send()
+                if i >= DIRECT:
+                    relay(first + u, u, i).wait_send()
 
     @pl.when(jnp.logical_and(inner, jnp.logical_not(near)))
     def _():
@@ -490,9 +610,10 @@
     rows = group * block_rows
     half_rows = rows // 2
     quarter = held // PARTS
+    units = per_half - 1 + CHUNKS
     bf16, f32 = jnp.bfloat16, jnp.float32
     dma = pltpu.SemaphoreType.DMA
-    anywhere = pl.BlockSpec(memory_space=pl.ANY)
+    held_in = pl.BlockSpec(memory_space=pltpu.HBM)
     vmem = pl.BlockSpec(memory_space=pltpu.VMEM)
     return pl.pallas_call(
         kernel,
@@ -500,13 +621,15 @@
             jax.ShapeDtypeStruct((prompts, block_rows, rows), f32),
             jax.ShapeDtypeStruct((prompts, block_rows), f32),
         ),
-        in_specs=[anywhere, anywhere, vmem],
+        in_specs=[held_in, held_in, held_in],
         out_specs=(vmem, vmem),
         scratch_shapes=[
+            pltpu.VMEM((prompts, block_rows), jnp.int32),
             pltpu.VMEM((per_half, group, block_rows, features), bf16),
             pltpu.VMEM((side, held, features), bf16),
             pltpu.VMEM((CORES, held, features // CHIPS), bf16),
             pltpu.VMEM((per_half, side, held, rows), bf16),
+            pltpu.VMEM((side, held, rows), f32),
             pltpu.VMEM((rows, rows), f32),
             pltpu.VMEM((per_half, half_rows, rows), f32),
             pltpu.VMEM((per_half, half_rows, rows), f32),
@@ -515,12 +638,13 @@
             pltpu.VMEM((prompts, block_rows, rows), bf16),
             pltpu.VMEM((prompts, 128), jnp.int32),
             pltpu.VMEM((group, prompts, 128), jnp.int32),
+            dma((1,)),
             dma((group - 1,)),
             dma((group,)),
-            dma((2, per_half)),
-            dma((per_half, group)),
+            dma((2, units)),
+            dma((units, group)),
             dma((per_half,)),
-            dma((per_half, 3)),
+            dma((units, 3)),
             dma((per_half,)),
             dma((4,)),
             dma((4,)),
@@ -538,7 +662,7 @@
             dma((prompts,)),
         ],
         compiler_params=pltpu.CompilerParams(
-            collective_id=0, has_side_effects=True, vmem_limit_bytes=56 << 20
+            collective_id=0, has_side_effects=True, vmem_limit_bytes=53 << 20
         ),
     )(embeddings, head_weight, mask)
 

time: 100 us -> 96 us (0.960)
  Pallas kernels: 96.6 us -> 93.2 us
    pallas_call x1, Pallas kernels: 96.6 us -> 93.2 us  [line_scores(): pl.pallas_call(kernel, out_shape=(jax.ShapeDtypeStruct((prompts, block_ro...]
    unnamed x2 -> x4, local copies, waits for them, and re-layouts: 2.95 us -> 1.98 us
where the time goes in v3:
time: 96 us; the launch traced here: 95.9 us
  Pallas kernels  93.2 us (97%)
  local copies, waits for them, and re-layouts  1.98 us (2%)
    pallas_call x1, Pallas kernels, line_scores(): pl.pallas_call(kernel, out_shape=(jax.ShapeDtypeStruct((prompts, block_ro...  93.2 us
    unnamed x4, local copies, waits for them, and re-layouts  1.98 us

profile of v3, /device:TPU:0, one launch (start us, length us, event | category | flops | bytes accessed | tf_op | source)
XLA Modules:
  0.0 95.9 jit_solution(9507032380702103671)
XLA Ops:
  0.6 0.0 copy-start
  0.6 0.7 copy-done
  1.3 93.2 %shard_map.50 = (f32[8,32,256]{2,1,0:T(8,128)S(1)}, f32[8,32]{1,0:T(8,128)S(1)}) custom-call(bf16[8,32,3584]{2,1,0:T(8,128)(2,1)} %e_ref.1, bf16[448,3584]{1,0:T(8,128)(2,1)} %w_ref.1, s32[8,32]{1,0:T(8,128)S(1)} %copy-done), custom_call_target="tpu_custom_call" | custom-call | tf_op jit(solution)/shard_map/pallas_call | solution.py:618
  94.6 0.7 copy.7
  95.3 0.6 copy.8
Async XLA Ops:
  0.6 0.7 copy-start

commit v4 on v3

v4 whole, which is shorter than its diff:
```python
import functools

import jax
import jax.numpy as jnp
from jax import lax
from jax.experimental import pallas as pl
from jax.experimental.pallas import tpu as pltpu
from jax.sharding import PartitionSpec as P

MESH = pl.DeviceIdType.MESH
CORES = 2
CHIPS = 4
PARTS = 4
CHUNKS = 2
DIRECT = 3
NT = (((1,), (1,)), ((), ()))


def gathered_halves(embeddings, head_weight, own_index, group_size):
    prompts, block_rows, features = embeddings.shape
    held = head_weight.shape[0]
    slots = group_size * block_rows
    everyone = lax.all_gather(embeddings, "resp", axis=0, tiled=True)
    flat = everyone.reshape(group_size * prompts * block_rows, features)
    through = lax.dot_general(flat, head_weight, NT, preferred_element_type=jnp.float32)
    through = through.astype(jnp.bfloat16).reshape(group_size, prompts, block_rows, held)
    mine = lax.dynamic_slice_in_dim(
        everyone.reshape(group_size, prompts, block_rows, features), own_index * held, held, 3
    )
    partial = jnp.einsum("gpid,hpjd->gpihj", mine, through, preferred_element_type=jnp.float32)
    flipped = jnp.einsum("gpid,hpjd->gpihj", through, mine, preferred_element_type=jnp.float32)
    partial = (partial - flipped).astype(jnp.bfloat16)
    return partial.reshape(group_size, prompts, block_rows, slots)


def gathered_scores(embeddings, head_weight):
    group_size = lax.axis_size("resp")
    own_index = lax.axis_index("resp")
    prompts, block_rows, features = embeddings.shape
    slots = group_size * block_rows
    at_once = max(1, min(prompts, (1 << 11) // slots))

    def scores_of(some):
        partial = gathered_halves(some, head_weight, own_index, group_size)
        swapped = lax.all_to_all(partial, "resp", split_axis=0, concat_axis=0, tiled=True)
        return jnp.sum(swapped.astype(jnp.float32), axis=0)

    pieces = embeddings.reshape(prompts // at_once, at_once, block_rows, features)
    return lax.map(scores_of, pieces).reshape(prompts, block_rows, slots)


def kernel(e_ref, w_ref, m_hbm, o_ref, r_ref,
           m_ref, ebuf, wbuf, gbuf, cbuf, zt, zsum, sbuf, keep, pbuf, qbuf, fbuf, rbuf, mine, mbuf,
           m_sems, e_send, e_recv, h_recv, n_sems, h_send, o_send, l_sems, g_send, g_recv,
           x_send, y_send, u_send, v_send, a_recv, b_recv, d_recv, p_send, p_recv, r_send, r_recv):
    part = lax.axis_index("prompt")
    me = lax.axis_index("resp")
    z = me // CORES
    core = me % CORES
    half = z // 2
    prompts, block_rows, features = e_ref.shape
    held = w_ref.shape[0]
    group = CHIPS * CORES
    per_half = prompts // 2
    side = group // 2
    span = held * side
    rows = group * block_rows
    half_rows = rows // 2
    quarter = held // PARTS
    z_in = 1 + half
    z_out = 3 * half
    z_far = 2 - half
    z_end = 3 - z_out
    inner = z == z_in
    near = core == half
    other = 1 - core
    here = me % side
    x_part = part + 1 - 2 * (part % 2)
    y_part = lax.rem(part + 2, PARTS)
    d_part = PARTS - 1 - part
    chip_width = features // CHIPS
    chunk_width = features // CHUNKS
    cut = held // 128 * 128
    spare = held - cut
    wide = chip_width - cut
    step = quarter // 7
    last = per_half - 1
    pieces = ((0, step), (step, 2 * step), (3 * step, 2 * step), (5 * step, 2 * step))
    count = len(pieces)
    direct = pieces[DIRECT][0]

    def copy(src, dst, send, recv, chip, c, q=None):
        return pltpu.make_async_remote_copy(
            src, dst, send, recv,
            device_id=(part if q is None else q, chip * CORES + c), device_id_type=MESH,
        )

    def arrived(dst, recv):
        copy(dst, dst, m_sems.at[0], recv, z_far, core).wait_recv()

    def departed(src, send):
        copy(src, src, send, m_sems.at[1], z_far, core).wait_send()

    m_copy = pltpu.make_async_copy(m_hbm, m_ref, m_sems.at[2])
    m_copy.start()
    others = [lax.rem(me + d, group) for d in range(1, group)]
    barrier = pltpu.get_barrier_semaphore()
    for peer in others:
        pl.semaphore_signal(barrier, inc=1, device_id=(part, peer), device_id_type=MESH)
    for q in (x_part, y_part):
        pl.semaphore_signal(barrier, inc=1, device_id=(q, me), device_id_type=MESH)

    def mask_copy(d):
        return pltpu.make_async_remote_copy(
            mine, mbuf.at[me], m_sems.at[0], m_sems.at[1],
            device_id=(part, others[d]), device_id_type=MESH,
        )

    def chip_cols(chip):
        return pl.ds(pl.multiple_of(chip * chip_width, 128), chip_width)

    def cut_cols(chip, h):
        return pl.ds(pl.multiple_of(chip * chip_width + h * wide, 128), cut)

    def weights(h, within, v):
        size = features - (chip_width if within else 0) - (cut if v else 0)
        block = 2 * ((1 - h) if within else h) + ((1 - h) if v else h)
        return block, pl.ds(pl.multiple_of((1 - h) * (features - size), 128), size)

    outer_set = tuple(weights(core, False, v) for v in range(2))
    inner_set = tuple(weights(core, True, v) for v in range(2))
    first = 2 * half
    every = pl.ds(0, features)

    def span_rows(q, i):
        at, size = pieces[i]
        return pl.ds(pl.multiple_of(q * quarter + at, 16), size)

    def outer_w(i, v):
        block, cols = weights(half, False, v)
        at = span_rows(part, i)
        dst = wbuf.at[block, at, cols]
        return copy(w_ref.at[at, cols] if v else dst, dst, o_send.at[0], a_recv.at[block, i], z_in, half)

    def outer_diag(v):
        block, cols = weights(half, False, v)
        at = pl.ds(pl.multiple_of(d_part * quarter, 16), direct)
        dst = wbuf.at[block, at, cols]
        return copy(w_ref.at[at, cols] if v else dst, dst, o_send.at[1], d_recv.at[block], z_in, half)

    def far_w(i, v):
        block, cols = weights(half, True, v)
        at = span_rows(part, i)
        dst = wbuf.at[block, at, cols]
        return copy(w_ref.at[at, cols] if v else dst, dst, o_send.at[0], a_recv.at[block, i], z_far, half)

    def near_w():
        block, cols = weights(half, True, 1)
        return copy(w_ref.at[:, cols], wbuf.at[block, :, cols], g_send.at[0], g_recv.at[2], z_in, half)

    def near_g():
        return copy(w_ref.at[:, chip_cols(z_out)], gbuf.at[core], g_send.at[1], g_recv.at[0], z_in, half)

    def near_c():
        at = pl.ds(pl.multiple_of((1 - half) * spare, 16), held)
        return copy(w_ref.at[:, cut_cols(z, half)], cbuf.at[at], g_send.at[2], g_recv.at[1], z, half)

    def own_w(within):
        block, cols = weights(half, within, 0)
        return pltpu.make_async_copy(w_ref.at[:, cols], wbuf.at[block, :, cols], l_sems.at[0])

    def own_g():
        return pltpu.make_async_copy(w_ref.at[:, chip_cols(z_out)], gbuf.at[core], l_sems.at[1])

    def fold_core():
        arrived(cbuf.at[pl.ds(0, held)], g_recv.at[1])
        row = lax.broadcasted_iota(jnp.int32, (held, cut), 0)
        col = lax.broadcasted_iota(jnp.int32, (held, cut), 1)
        pick = (row - half * spare == col).astype(jnp.bfloat16)
        turned = lax.dot_general(pick, cbuf[...], NT, preferred_element_type=jnp.float32)
        cols = pl.ds(pl.multiple_of(z * chip_width + (1 - half) * cut, 128), wide)
        wbuf[here, :, cols] = (wbuf[here, :, cols].astype(jnp.float32) - turned).astype(jnp.bfloat16)

    def fold(q, at, size):
        start = q * quarter + at
        row = lax.broadcasted_iota(jnp.int32, (2 * size, chip_width), 0)
        col = lax.broadcasted_iota(jnp.int32, (2 * size, chip_width), 1)
        pick = (start + jnp.where(row < size, row, row + held - size) == col).astype(jnp.bfloat16)
        turned = lax.dot_general(
            pick, gbuf[...].reshape(chip_width, chip_width), NT, preferred_element_type=jnp.float32
        ).reshape(2, size, chip_width)
        pair, where, cols = pl.ds(first, 2), pl.ds(pl.multiple_of(start, 16), size), chip_cols(z_in)
        wbuf[pair, where, cols] = (wbuf[pair, where, cols].astype(jnp.float32) - turned).astype(jnp.bfloat16)

    def got_mine(w, i):
        block, cols = w
        arrived(wbuf.at[block, span_rows(part, i), cols], a_recv.at[block, i])

    def got_sides(w, i):
        block, cols = w
        arrived(wbuf.at[block, pl.ds(0, 2 * pieces[i][1]), cols], b_recv.at[block, i])

    def got_diag(w):
        block, cols = w
        arrived(wbuf.at[block, pl.ds(0, quarter), cols], d_recv.at[block])

    def along(w, q, i, send, recv, chip, q_to):
        block, cols = w
        spot = wbuf.at[block, span_rows(q, i), cols]
        return copy(spot, spot, send, recv, chip, core, q_to)

    def spread(w, i):
        along(w, part, i, x_send.at[w[0]], b_recv.at[w[0], i], z_in, x_part).start()
        along(w, part, i, y_send.at[w[0]], b_recv.at[w[0], i], z_in, y_part).start()

    def to_far(w, i):
        along(w, part, i, u_send.at[w[0]], a_recv.at[w[0], i], z_far, part).start()

    def relay(w, v, i):
        got_sides(w, i)
        if (i < 2) == (v == 0):
            along(w, x_part, i, v_send.at[w[0]], d_recv.at[w[0]], z_in, y_part).start()
        else:
            along(w, y_part, i, v_send.at[w[0]], d_recv.at[w[0]], z_in, x_part).start()

    def sent_rows(w, send, many):
        block, cols = w
        departed(wbuf.at[block, pl.ds(0, many), cols], send.at[block])

    def chunk_cols(k):
        return pl.ds(pl.multiple_of(k * chunk_width, 128), chunk_width)

    def e_part(j, block, k):
        if k is None:
            return ebuf.at[j, block]
        return ebuf.at[j, block, :, chunk_cols(k)]

    def e_mine(h, j, k):
        if k is None:
            return e_ref.at[h * per_half + j]
        return e_ref.at[h * per_half + j, :, chunk_cols(k)]

    def unit(j, k):
        return j if k is None else j + k

    def e_far(j, k=None):
        return copy(e_mine(1 - half, j, k), e_part(j, me, k), e_send.at[1], e_recv.at[unit(j, k)], z_far, core)

    def e_near(j, k=None):
        return copy(e_mine(half, j, k), e_part(j, me, k), e_send.at[0], e_recv.at[unit(j, k)], z_in, core)

    def near_e(j):
        return copy(e_mine(half, j, None), ebuf.at[j, me], n_sems.at[0], n_sems.at[1], z_in, other)

    def own_e(j):
        return pltpu.make_async_copy(e_mine(half, j, None), ebuf.at[j, me], n_sems.at[2])

    away = (z_out, z_far, z_end)

    def three(j, k):
        if k is None:
            return ebuf.at[j, pl.ds(0, 3)]
        return ebuf.at[j, pl.ds(0, 3), :, chunk_cols(k)]

    def take_e(j, k=None):
        arrived(three(j, k), e_recv.at[unit(j, k)])
        for chip in away:
            spot = e_part(j, chip * CORES + core, k)
            copy(spot, spot, h_send.at[0], h_recv.at[unit(j, k)], z_in, other).start()

    def have_e(j, k=None):
        arrived(three(j, k), h_recv.at[unit(j, k)])

    def have_own():
        pltpu.make_async_copy(ebuf.at[:, me], ebuf.at[:, me], n_sems.at[2]).wait()
        arrived(ebuf.at[:, z_in * CORES + other], n_sems.at[1])

    def all_units(act):
        for j in range(last):
            act(j, None)
        for k in range(CHUNKS):
            act(last, k)

    def partial_copy(j):
        return copy(pbuf.at[j], qbuf.at[j], p_send.at[0], p_recv.at[j], z_in, other)

    def project(q, j):
        at = pl.ds(pl.multiple_of(q * quarter, 16), quarter)
        left = wbuf[:, at].reshape(side * quarter, features)
        right = ebuf[j].reshape(rows, features)
        zt[j, :, at] = lax.dot_general(
            left, right, NT, preferred_element_type=jnp.float32
        ).astype(jnp.bfloat16).reshape(side, quarter, rows)

    def project_last(q, k):
        at = pl.ds(pl.multiple_of(q * quarter, 16), quarter)
        cols = chunk_cols(k)
        left = wbuf[:, at, cols].reshape(side * quarter, chunk_width)
        right = ebuf[last, :, :, cols].reshape(rows, chunk_width)
        total = lax.dot_general(
            left, right, NT, preferred_element_type=jnp.float32
        ).reshape(side, quarter, rows)
        total = jnp.where(k > 0, zsum[:, at], 0.0) + total
        zsum[:, at] = total
        zt[last, :, at] = total.astype(jnp.bfloat16)

    lanes = pl.ds(pl.multiple_of(core * span, 128), span)
    mine_at = pl.multiple_of(core * half_rows, half_rows)
    theirs_at = pl.multiple_of(other * half_rows, half_rows)

    def score(j):
        left = ebuf[j, :, :, lanes].reshape(rows, span)
        raw = jnp.dot(left, zt[j].reshape(span, rows), preferred_element_type=jnp.float32)
        sbuf[...] = raw - jnp.transpose(raw)
        pbuf[j] = sbuf[pl.ds(theirs_at, half_rows)]
        partial_copy(j).start()
        keep[j] = sbuf[pl.ds(mine_at, half_rows)]

    def final_copy(j, t):
        row = pl.multiple_of(t * block_rows, block_rows)
        return pltpu.make_async_remote_copy(
            fbuf.at[j, pl.ds(row, block_rows)], rbuf.at[half * per_half + j],
            r_send.at[0], r_recv.at[half, j // last],
            device_id=(part, core * side + t), device_id_type=MESH,
        )

    def finish(j):
        arrived(qbuf.at[j], p_recv.at[j])
        fbuf[j] = (keep[j] + qbuf[j]).astype(jnp.bfloat16)
        for t in range(side):
            @pl.when(core * side + t != me)
            def _():
                final_copy(j, t).start()

        @pl.when(near)
        def _():
            row = pl.multiple_of(here * block_rows, block_rows)
            rbuf[half * per_half + j] = fbuf[j, pl.ds(row, block_rows)]

    def each_mask():
        for d in range(group - 1):
            mask_copy(d).start()

    def loop(n, body):
        def run(j, carry):
            body(j)
            return carry
        lax.fori_loop(0, n, run, 0)

    def choose(index, values):
        picked = values[0]
        for n in range(1, len(values)):
            picked = jnp.where(index == n, values[n], picked)
        return picked

    quarters = (part, x_part, y_part, d_part)

    @pl.when(near)
    def _():
        @pl.when(inner)
        def _():
            own_w(True).start()
            own_g().start()

        @pl.when(jnp.logical_not(inner))
        def _():
            own_w(False).start()

    @pl.when(inner)
    def _():
        for j in range(per_half):
            own_e(j).start()

    wbuf[pl.ds(inner_set[0][0] // 2 * 2, 2), :, chip_cols(3 * core)] = jnp.zeros((2, held, chip_width), jnp.bfloat16)
    wbuf[inner_set[1][0], :, cut_cols(1 + core, core)] = jnp.zeros((held, cut), jnp.bfloat16)
    wbuf[outer_set[1][0], :, cut_cols(3 * core, core)] = jnp.zeros((held, cut), jnp.bfloat16)
    cbuf[pl.ds(pl.multiple_of(half * held, 16), spare)] = jnp.zeros((spare, cut), jnp.bfloat16)
    m_copy.wait()
    valid = m_ref[...].astype(jnp.float32)
    mine[...] = jnp.broadcast_to(jnp.sum(m_ref[...], axis=1, keepdims=True), mine.shape)
    pl.semaphore_wait(barrier, len(others) + 2)

    for v in range(2):
        @pl.when(jnp.logical_and(jnp.logical_not(inner), near == (v == 0)))
        def _():
            if v:
                near_c().start()
            else:
                own_w(False).wait()
                fold_core()
            for i in range(count):
                outer_w(i, v).start()
            each_mask()
            outer_diag(v).start()

            def send(j, k):
                e_near(j, k).start()
                e_far(j, k).start()

            all_units(send)

    @pl.when(jnp.logical_and(inner, near))
    def _():
        own_w(True).wait()
        fold_core()
        for i in range(count):
            far_w(i, 0).start()
        each_mask()
        for j in range(per_half):
            near_e(j).start()
        own_g().wait()
        arrived(gbuf.at[other], g_recv.at[0])
        for i in range(count):
            for w in outer_set:
                got_mine(w, i)
            fold(part, *pieces[i])
            for w in outer_set:
                to_far(w, i)
                spread(w, i)
        all_units(lambda j, k: e_far(j, k).start())
        block, cols = weights(half, True, 1)
        arrived(wbuf.at[block, :, cols], g_recv.at[2])
        have_own()
        for i in range(count):
            for v in range(2):
                if i < DIRECT:
                    got_sides(outer_set[v], i)
                else:
                    relay(outer_set[v], v, i)

        def turn(t):
            j = t // PARTS
            s = t % PARTS

            @pl.when(s == 0)
            def _():
                take_e(j)
                have_e(j)

            @pl.when(t == PARTS - 1)
            def _():
                for w in outer_set:
                    got_diag(w)
                fold(d_part, 0, direct)

            @pl.when(t == last * PARTS - 3)
            def _():
                take_e(last, 0)
            project(choose(s, quarters), j)

            @pl.when(s == PARTS - 1)
            def _():
                score(j)

        loop(last * PARTS, turn)

        def final_turn(n):
            k = n // PARTS
            s = n % PARTS

            @pl.when(s == 0)
            def _():
                @pl.when(k < CHUNKS - 1)
                def _():
                    take_e(last, k + 1)

                have_e(last, k)
            project_last(choose(s, quarters), k)

        loop(CHUNKS * PARTS, final_turn)
        loop(last, finish)
        score(last)
        finish(last)

    @pl.when(jnp.logical_and(inner, jnp.logical_not(near)))
    def _():
        near_c().start()
        near_g().start()
        for i in range(count):
            far_w(i, 1).start()
        each_mask()
        near_w().start()
        for j in range(per_half):
            near_e(j).start()
        for pair in (inner_set, outer_set):
            for i in range(count):
                for w in pair:
                    got_mine(w, i)
                    spread(w, i)
        all_units(lambda j, k: e_far(j, k).start())
        for i in range(count):
            for v in range(2):
                relay(inner_set[v], v, i)
        have_own()
        take_e(0)
        have_e(0)
        order = ((0, 0), (1, 0), (2, 0), (0, 1), (1, 1), (2, 1), (0, 2), (1, 2), (2, 2), (3, 0), (3, 1), (3, 2))

        def turn(t):
            what = choose(t, [q * PARTS + j for q, j in order])

            @pl.when(t == 1)
            def _():
                for i in range(count):
                    if i == count - 1:
                        take_e(1)
                    for v in range(2):
                        relay(outer_set[v], v, i)

            @pl.when(t == 3)
            def _():
                have_e(1)

            @pl.when(t == 6)
            def _():
                take_e(2)
                have_e(2)

            @pl.when(t == 9)
            def _():
                take_e(last, 0)
                for w in inner_set + outer_set:
                    got_diag(w)
            project(choose(what // PARTS, quarters), what % PARTS)

        loop(len(order), turn)
        have_e(last, 0)

        def final_turn(n):
            @pl.when(n == PARTS)
            def _():
                take_e(last, 1)
                loop(last, score)
                loop(last, finish)
                have_e(last, 1)
            project_last(choose(n % PARTS, quarters), n // PARTS)

        loop(CHUNKS * PARTS, final_turn)
        score(last)
        finish(last)

    arrived(mbuf.at[pl.ds(0, group - 1)], m_sems.at[1])
    mbuf[me] = mine[...]
    counts = mbuf[0]
    for g in range(1, group):
        counts = counts + mbuf[g]
    counts = counts[:, :1].astype(jnp.float32)
    slot = lax.broadcasted_iota(jnp.int32, (prompts, rows), 1).astype(jnp.float32)
    cols = (slot < counts).astype(jnp.float32)
    pairs = jnp.maximum(counts - 1.0, 1.0)
    same = lax.broadcasted_iota(jnp.int32, (block_rows, block_rows), 0)
    same = (same == lax.broadcasted_iota(jnp.int32, (block_rows, block_rows), 1)).astype(jnp.float32)
    down = lax.dot_general(same, valid, NT, preferred_element_type=jnp.float32)
    lane = lax.broadcasted_iota(jnp.int32, (block_rows, 128), 1)
    rates = jnp.zeros((block_rows, 128), jnp.float32)
    for batch in (range(last), range(last, per_half)):
        for h in range(2):
            @pl.when(jnp.logical_not(jnp.logical_and(jnp.logical_and(inner, near), half == h)))
            def _():
                arrived(rbuf.at[pl.ds(h * per_half + batch[0], len(batch))], r_recv.at[h, batch[0] // last])
        for j in batch:
            for h in range(2):
                p = h * per_half + j
                given = down[:, p:p + 1]
                prefs = jax.nn.sigmoid(rbuf[p].astype(jnp.float32)) * given * cols[p:p + 1, :]
                o_ref[p] = prefs
                totals = jnp.sum(prefs, axis=1, keepdims=True) - 0.5 * given
                rates = jnp.where(lane == p, given * totals / pairs[p:p + 1, :], rates)
    r_ref[...] = jnp.transpose(rates)[:prompts]

    departed(mbuf.at[pl.ds(0, group - 1)], m_sems.at[0])
    departed(ebuf.at[:, 0], e_send.at[1])
    for v in range(2):
        @pl.when(near == (v == 0))
        def _():
            @pl.when(inner)
            def _():
                block, cols = weights(half, True, v)
                departed(wbuf.at[block, pl.ds(0, quarter), cols], o_send.at[0])

            @pl.when(jnp.logical_not(inner))
            def _():
                block, cols = weights(half, False, v)
                departed(wbuf.at[block, pl.ds(0, quarter), cols], o_send.at[0])
                departed(wbuf.at[block, pl.ds(0, direct), cols], o_send.at[1])

    @pl.when(jnp.logical_not(near))
    def _():
        near_c().wait_send()

    @pl.when(jnp.logical_not(inner))
    def _():
        departed(ebuf.at[:, 0], e_send.at[0])

    @pl.when(inner)
    def _():
        departed(ebuf.at[:, 0], n_sems.at[0])
        departed(ebuf.at[:, pl.ds(0, 3)], h_send.at[0])
        departed(pbuf, p_send.at[0])

    @pl.when(jnp.logical_and(inner, near))
    def _():
        for w in outer_set:
            for sems in (x_send, y_send, u_send):
                sent_rows(w, sems, quarter)
            sent_rows(w, v_send, quarter - direct)
        departed(fbuf.at[:, pl.ds(0, half_rows - block_rows)], r_send.at[0])

    @pl.when(jnp.logical_and(inner, jnp.logical_not(near)))
    def _():
        near_g().wait_send()
        near_w().wait_send()
        for w in inner_set + outer_set:
            for sems in (x_send, y_send, v_send):
                sent_rows(w, sems, quarter)
        departed(fbuf, r_send.at[0])


def line_scores(embeddings, head_weight, mask):
    prompts, block_rows, features = embeddings.shape
    held = head_weight.shape[0]
    group = CHIPS * CORES
    side = group // 2
    per_half = prompts // 2
    rows = group * block_rows
    half_rows = rows // 2
    units = per_half - 1 + CHUNKS
    chip_width = features // CHIPS
    cut = held // 128 * 128
    bf16, f32 = jnp.bfloat16, jnp.float32
    dma = pltpu.SemaphoreType.DMA
    held_in = pl.BlockSpec(memory_space=pltpu.HBM)
    vmem = pl.BlockSpec(memory_space=pltpu.VMEM)
    return pl.pallas_call(
        kernel,
        out_shape=(
            jax.ShapeDtypeStruct((prompts, block_rows, rows), f32),
            jax.ShapeDtypeStruct((prompts, block_rows), f32),
        ),
        in_specs=[held_in, held_in, held_in],
        out_specs=(vmem, vmem),
        scratch_shapes=[
            pltpu.VMEM((prompts, block_rows), jnp.int32),
            pltpu.VMEM((per_half, group, block_rows, features), bf16),
            pltpu.VMEM((side, held, features), bf16),
            pltpu.VMEM((CORES, held, chip_width), bf16),
            pltpu.VMEM((chip_width - cut, cut), bf16),
            pltpu.VMEM((per_half, side, held, rows), bf16),
            pltpu.VMEM((side, held, rows), f32),
            pltpu.VMEM((rows, rows), f32),
            pltpu.VMEM((per_half, half_rows, rows), f32),
            pltpu.VMEM((per_half, half_rows, rows), f32),
            pltpu.VMEM((per_half, half_rows, rows), f32),
            pltpu.VMEM((per_half, half_rows, rows), bf16),
            pltpu.VMEM((prompts, block_rows, rows), bf16),
            pltpu.VMEM((prompts, 128), jnp.int32),
            pltpu.VMEM((group, prompts, 128), jnp.int32),
            dma((3,)),
            dma((2,)),
            dma((units,)),
            dma((units,)),
            dma((3,)),
            dma((1,)),
            dma((2,)),
            dma((2,)),
            dma((3,)),
            dma((3,)),
            dma((side,)),
            dma((side,)),
            dma((side,)),
            dma((side,)),
            dma((side, 4)),
            dma((side, 4)),
            dma((side,)),
            dma((1,)),
            dma((per_half,)),
            dma((1,)),
            dma((2, 2)),
        ],
        compiler_params=pltpu.CompilerParams(
            collective_id=0, has_side_effects=True, vmem_limit_bytes=53 << 20
        ),
    )(embeddings, head_weight, mask)


def shards(embeddings, head_weight, valid_mask):
    group_size = lax.axis_size("resp")
    slots = group_size * embeddings.shape[1]
    if (lax.axis_size("prompt"), group_size) == (PARTS, CHIPS * CORES):
        return line_scores(embeddings, head_weight, valid_mask)
    valid_rows = valid_mask.astype(jnp.float32)
    counts = lax.psum(jnp.sum(valid_rows, axis=1), "resp")
    scores = gathered_scores(embeddings, head_weight)
    column_ids = jnp.arange(slots, dtype=jnp.float32)
    valid_cols = (column_ids[None, :] < counts[:, None]).astype(jnp.float32)
    preferences = jax.nn.sigmoid(scores) * valid_rows[:, :, None] * valid_cols[:, None, :]
    totals = jnp.sum(preferences, axis=2) - 0.5 * valid_rows
    win_rates = valid_rows * totals / jnp.maximum(counts - 1.0, 1.0)[:, None]
    return (preferences, win_rates)


def solution(mesh):
    return jax.shard_map(
        shards,
        mesh=mesh,
        in_specs=(P("prompt", "resp", None), P("resp", None), P("prompt", "resp")),
        out_specs=(P("prompt", "resp", None), P("prompt", "resp")),
        check_vma=False,
    )
```

time: 96 us -> 93.8 us (0.977)
  Pallas kernels: 93.2 us -> 91 us
    pallas_call x1, Pallas kernels: 93.2 us -> 91 us  [line_scores(): pl.pallas_call(kernel, out_shape=(jax.ShapeDtypeStruct((prompts, block_ro...]
where the time goes in v4:
time: 93.8 us; the launch traced here: 93.6 us
  Pallas kernels  91 us (97%)
  local copies, waits for them, and re-layouts  1.98 us (2%)
    pallas_call x1, Pallas kernels, line_scores(): pl.pallas_call(kernel, out_shape=(jax.ShapeDtypeStruct((prompts, block_ro...  91 us
    unnamed x4, local copies, waits for them, and re-layouts  1.98 us

profile of v4, /device:TPU:0, one launch (start us, length us, event | category | flops | bytes accessed | tf_op | source)
XLA Modules:
  0.0 93.6 jit_solution(14042350872555695782)
XLA Ops:
  0.6 0.0 copy-start
  0.6 0.7 copy-done
  1.3 91.0 %shard_map.50 = (f32[8,32,256]{2,1,0:T(8,128)S(1)}, f32[8,32]{1,0:T(8,128)S(1)}) custom-call(bf16[8,32,3584]{2,1,0:T(8,128)(2,1)} %e_ref.1, bf16[448,3584]{1,0:T(8,128)(2,1)} %w_ref.1, s32[8,32]{1,0:T(8,128)S(1)} %copy-done), custom_call_target="tpu_custom_call" | custom-call | tf_op jit(solution)/shard_map/pallas_call | solution.py:634
  92.3 0.7 copy.7
  93.0 0.6 copy.8
Async XLA Ops:
  0.6 0.7 copy-start

commit v5 on v4

--- a/solution.py
+++ b/solution.py
@@ -50,9 +50,9 @@
 
 
 def kernel(e_ref, w_ref, m_hbm, o_ref, r_ref,
-           m_ref, ebuf, wbuf, gbuf, cbuf, zt, zsum, sbuf, keep, pbuf, qbuf, fbuf, rbuf, mine, mbuf,
+           m_ref, ebuf, wbuf, gbuf, cbuf, zt, zfar, zsum, held_raw, sbuf, keep, pbuf, qbuf, fbuf, tbuf, rbuf, mine, mbuf,
            m_sems, e_send, e_recv, h_recv, n_sems, h_send, o_send, l_sems, g_send, g_recv,
-           x_send, y_send, u_send, v_send, a_recv, b_recv, d_recv, p_send, p_recv, r_send, r_recv):
+           x_send, y_send, u_send, v_send, a_recv, b_recv, d_recv, z_send, z_recv, p_send, p_recv, r_send, r_recv):
     part = lax.axis_index("prompt")
     me = lax.axis_index("resp")
     z = me // CORES
@@ -79,7 +79,9 @@
     y_part = lax.rem(part + 2, PARTS)
     d_part = PARTS - 1 - part
     chip_width = features // CHIPS
-    chunk_width = features // CHUNKS
+    tiles = features // 256
+    ends = [tiles * (CHUNKS - k) // CHUNKS * 256 for k in range(CHUNKS)]
+    chunks = [(features - end, end - after) for end, after in zip(ends, ends[1:] + [0])]
     cut = held // 128 * 128
     spare = held - cut
     wide = chip_width - cut
@@ -228,7 +230,7 @@
         departed(wbuf.at[block, pl.ds(0, many), cols], send.at[block])
 
     def chunk_cols(k):
-        return pl.ds(pl.multiple_of(k * chunk_width, 128), chunk_width)
+        return pl.ds(*chunks[k])
 
     def e_part(j, block, k):
         if k is None:
@@ -244,10 +246,11 @@
         return j if k is None else j + k
 
     def e_far(j, k=None):
-        return copy(e_mine(1 - half, j, k), e_part(j, me, k), e_send.at[1], e_recv.at[unit(j, k)], z_far, core)
+        recv = e_recv.at[unit(j, k), z]
+        return copy(e_mine(1 - half, j, k), e_part(j, me, k), e_send.at[1], recv, z_far, core)
 
     def e_near(j, k=None):
-        return copy(e_mine(half, j, k), e_part(j, me, k), e_send.at[0], e_recv.at[unit(j, k)], z_in, core)
+        return copy(e_mine(half, j, k), e_part(j, me, k), e_send.at[0], e_recv.at[unit(j, k), z], z_in, core)
 
     def near_e(j):
         return copy(e_mine(half, j, None), ebuf.at[j, me], n_sems.at[0], n_sems.at[1], z_in, other)
@@ -263,9 +266,9 @@
         return ebuf.at[j, pl.ds(0, 3), :, chunk_cols(k)]
 
     def take_e(j, k=None):
-        arrived(three(j, k), e_recv.at[unit(j, k)])
         for chip in away:
             spot = e_part(j, chip * CORES + core, k)
+            arrived(spot, e_recv.at[unit(j, k), chip])
             copy(spot, spot, h_send.at[0], h_recv.at[unit(j, k)], z_in, other).start()
 
     def have_e(j, k=None):
@@ -281,8 +284,11 @@
         for k in range(CHUNKS):
             act(last, k)
 
-    def partial_copy(j):
-        return copy(pbuf.at[j], qbuf.at[j], p_send.at[0], p_recv.at[j], z_in, other)
+    def partial_copy():
+        return copy(pbuf, qbuf, p_send.at[0], p_recv.at[0], z_in, other)
+
+    def far_copy(j):
+        return copy(zt.at[j], zfar.at[j], z_send.at[0], z_recv.at[j], z_in, other)
 
     def project(q, j):
         at = pl.ds(pl.multiple_of(q * quarter, 16), quarter)
@@ -294,48 +300,62 @@
 
     def project_last(q, k):
         at = pl.ds(pl.multiple_of(q * quarter, 16), quarter)
-        cols = chunk_cols(k)
-        left = wbuf[:, at, cols].reshape(side * quarter, chunk_width)
-        right = ebuf[last, :, :, cols].reshape(rows, chunk_width)
+        cols, width = chunk_cols(k), chunks[k][1]
+        left = wbuf[:, at, cols].reshape(side * quarter, width)
+        right = ebuf[last, :, :, cols].reshape(rows, width)
         total = lax.dot_general(
             left, right, NT, preferred_element_type=jnp.float32
         ).reshape(side, quarter, rows)
-        total = jnp.where(k > 0, zsum[:, at], 0.0) + total
-        zsum[:, at] = total
-        zt[last, :, at] = total.astype(jnp.bfloat16)
-
-    lanes = pl.ds(pl.multiple_of(core * span, 128), span)
+        if k > 0:
+            total = zsum[:, at] + total
+        if k < CHUNKS - 1:
+            zsum[:, at] = total
+        else:
+            zt[last, :, at] = total.astype(jnp.bfloat16)
+
     mine_at = pl.multiple_of(core * half_rows, half_rows)
     theirs_at = pl.multiple_of(other * half_rows, half_rows)
 
-    def score(j):
+    def raw_scores(j, c, held_zt):
+        lanes = pl.ds(pl.multiple_of(c * span, 128), span)
         left = ebuf[j, :, :, lanes].reshape(rows, span)
-        raw = jnp.dot(left, zt[j].reshape(span, rows), preferred_element_type=jnp.float32)
+        return jnp.dot(left, held_zt[j].reshape(span, rows), preferred_element_type=jnp.float32)
+
+    def score_last():
+        raw = raw_scores(last, core, zt)
         sbuf[...] = raw - jnp.transpose(raw)
-        pbuf[j] = sbuf[pl.ds(theirs_at, half_rows)]
-        partial_copy(j).start()
-        keep[j] = sbuf[pl.ds(mine_at, half_rows)]
-
-    def final_copy(j, t):
-        row = pl.multiple_of(t * block_rows, block_rows)
+        pbuf[...] = sbuf[pl.ds(theirs_at, half_rows)]
+        partial_copy().start()
+        keep[...] = sbuf[pl.ds(mine_at, half_rows)]
+
+    def block_at(t):
+        return pl.ds(pl.multiple_of(t * block_rows, block_rows), block_rows)
+
+    def final_copy(src, j, t):
         return pltpu.make_async_remote_copy(
-            fbuf.at[j, pl.ds(row, block_rows)], rbuf.at[half * per_half + j],
-            r_send.at[0], r_recv.at[half, j // last],
-            device_id=(part, core * side + t), device_id_type=MESH,
+            src, rbuf.at[half * per_half + j], r_send.at[0], r_recv.at[half, j // last],
+            device_id=(part, t), device_id_type=MESH,
         )
 
-    def finish(j):
-        arrived(qbuf.at[j], p_recv.at[j])
-        fbuf[j] = (keep[j] + qbuf[j]).astype(jnp.bfloat16)
+    def score_all(j):
+        arrived(zfar.at[j], z_recv.at[j])
+        raw = held_raw[j] + raw_scores(j, other, zfar)
+        fbuf[j] = (raw - jnp.transpose(raw)).astype(jnp.bfloat16)
+        for d in range(group - 1):
+            final_copy(fbuf.at[j, block_at(others[d])], j, others[d]).start()
+        rbuf[half * per_half + j] = fbuf[j, block_at(me)]
+
+    def finish_last():
+        arrived(qbuf, p_recv.at[0])
+        tbuf[...] = (keep[...] + qbuf[...]).astype(jnp.bfloat16)
         for t in range(side):
             @pl.when(core * side + t != me)
             def _():
-                final_copy(j, t).start()
+                final_copy(tbuf.at[block_at(t)], last, core * side + t).start()
 
         @pl.when(near)
         def _():
-            row = pl.multiple_of(here * block_rows, block_rows)
-            rbuf[half * per_half + j] = fbuf[j, pl.ds(row, block_rows)]
+            rbuf[half * per_half + last] = tbuf[block_at(here)]
 
     def each_mask():
         for d in range(group - 1):
@@ -450,27 +470,18 @@
 
             @pl.when(s == PARTS - 1)
             def _():
-                score(j)
+                held_raw[j] = raw_scores(j, core, zt)
 
         loop(last * PARTS, turn)
 
-        def final_turn(n):
-            k = n // PARTS
-            s = n % PARTS
-
-            @pl.when(s == 0)
-            def _():
-                @pl.when(k < CHUNKS - 1)
-                def _():
-                    take_e(last, k + 1)
-
-                have_e(last, k)
-            project_last(choose(s, quarters), k)
-
-        loop(CHUNKS * PARTS, final_turn)
-        loop(last, finish)
-        score(last)
-        finish(last)
+        for k in range(CHUNKS):
+            if k + 1 < CHUNKS:
+                take_e(last, k + 1)
+            have_e(last, k)
+            loop(PARTS, lambda s: project_last(choose(s, quarters), k))
+        loop(last, score_all)
+        score_last()
+        finish_last()
 
     @pl.when(jnp.logical_and(inner, jnp.logical_not(near)))
     def _():
@@ -519,25 +530,23 @@
             @pl.when(t == 9)
             def _():
                 take_e(last, 0)
+                have_e(last, 0)
+                loop(PARTS - 1, lambda s: project_last(choose(s, quarters), 0))
                 for w in inner_set + outer_set:
                     got_diag(w)
+                take_e(last, 1)
             project(choose(what // PARTS, quarters), what % PARTS)
 
+            @pl.when(t >= 9)
+            def _():
+                far_copy(t - 9).start()
+
         loop(len(order), turn)
-        have_e(last, 0)
-
-        def final_turn(n):
-            @pl.when(n == PARTS)
-            def _():
-                take_e(last, 1)
-                loop(last, score)
-                loop(last, finish)
-                have_e(last, 1)
-            project_last(choose(n % PARTS, quarters), n // PARTS)
-
-        loop(CHUNKS * PARTS, final_turn)
-        score(last)
-        finish(last)
+        project_last(d_part, 0)
+        have_e(last, 1)
+        loop(PARTS, lambda s: project_last(choose(s, quarters), 1))
+        score_last()
+        finish_last()
 
     arrived(mbuf.at[pl.ds(0, group - 1)], m_sems.at[1])
     mbuf[me] = mine[...]
@@ -604,7 +613,7 @@
             for sems in (x_send, y_send, u_send):
                 sent_rows(w, sems, quarter)
             sent_rows(w, v_send, quarter - direct)
-        departed(fbuf.at[:, pl.ds(0, half_rows - block_rows)], r_send.at[0])
+        departed(fbuf, r_send.at[0])
 
     @pl.when(jnp.logical_and(inner, jnp.logical_not(near)))
     def _():
@@ -613,7 +622,8 @@
         for w in inner_set + outer_set:
             for sems in (x_send, y_send, v_send):
                 sent_rows(w, sems, quarter)
-        departed(fbuf, r_send.at[0])
+        departed(zt.at[pl.ds(0, last)], z_send.at[0])
+        departed(tbuf, r_send.at[0])
 
 
 def line_scores(embeddings, head_weight, mask):
@@ -646,18 +656,21 @@
             pltpu.VMEM((CORES, held, chip_width), bf16),
             pltpu.VMEM((chip_width - cut, cut), bf16),
             pltpu.VMEM((per_half, side, held, rows), bf16),
+            pltpu.VMEM((per_half - 1, side, held, rows), bf16),
             pltpu.VMEM((side, held, rows), f32),
+            pltpu.VMEM((per_half - 1, rows, rows), f32),
             pltpu.VMEM((rows, rows), f32),
-            pltpu.VMEM((per_half, half_rows, rows), f32),
-            pltpu.VMEM((per_half, half_rows, rows), f32),
-            pltpu.VMEM((per_half, half_rows, rows), f32),
-            pltpu.VMEM((per_half, half_rows, rows), bf16),
+            pltpu.VMEM((half_rows, rows), f32),
+            pltpu.VMEM((half_rows, rows), f32),
+            pltpu.VMEM((half_rows, rows), f32),
+            pltpu.VMEM((per_half - 1, rows, rows), bf16),
+            pltpu.VMEM((half_rows, rows), bf16),
             pltpu.VMEM((prompts, block_rows, rows), bf16),
             pltpu.VMEM((prompts, 128), jnp.int32),
             pltpu.VMEM((group, prompts, 128), jnp.int32),
             dma((3,)),
             dma((2,)),
-            dma((units,)),
+            dma((units, CHIPS)),
             dma((units,)),
             dma((3,)),
             dma((1,)),
@@ -673,7 +686,9 @@
             dma((side, 4)),
             dma((side,)),
             dma((1,)),
-            dma((per_half,)),
+            dma((per_half - 1,)),
+            dma((1,)),
+            dma((1,)),
             dma((1,)),
             dma((2, 2)),
         ],

time: 93.8 us -> 91 us (0.970)
  Pallas kernels: 91 us -> 88.2 us
    pallas_call x1, Pallas kernels: 91 us -> 88.2 us  [line_scores(): pl.pallas_call(kernel, out_shape=(jax.ShapeDtypeStruct((prompts, block_ro...]
where the time goes in v5:
time: 91 us; the launch traced here: 90.8 us
  Pallas kernels  88.2 us (97%)
  local copies, waits for them, and re-layouts  1.98 us (2%)
    pallas_call x1, Pallas kernels, line_scores(): pl.pallas_call(kernel, out_shape=(jax.ShapeDtypeStruct((prompts, block_ro...  88.2 us
    unnamed x4, local copies, waits for them, and re-layouts  1.98 us

profile of v5, /device:TPU:0, one launch (start us, length us, event | category | flops | bytes accessed | tf_op | source)
XLA Modules:
  0.0 90.8 jit_solution(13347327160340480235)
XLA Ops:
  0.6 0.0 copy-start
  0.6 0.7 copy-done
  1.3 88.2 %shard_map.50 = (f32[8,32,256]{2,1,0:T(8,128)S(1)}, f32[8,32]{1,0:T(8,128)S(1)}) custom-call(bf16[8,32,3584]{2,1,0:T(8,128)(2,1)} %e_ref.1, bf16[448,3584]{1,0:T(8,128)(2,1)} %w_ref.1, s32[8,32]{1,0:T(8,128)S(1)} %copy-done), custom_call_target="tpu_custom_call" | custom-call | tf_op jit(solution)/shard_map/pallas_call | solution.py:644
  89.5 0.7 copy.7
  90.3 0.6 copy.8
Async XLA Ops:
  0.6 0.7 copy-start

commit v6 on v5

--- a/solution.py
+++ b/solution.py
@@ -87,6 +87,7 @@
     wide = chip_width - cut
     step = quarter // 7
     last = per_half - 1
+    whole = per_half - 2
     pieces = ((0, step), (step, 2 * step), (3 * step, 2 * step), (5 * step, 2 * step))
     count = len(pieces)
     direct = pieces[DIRECT][0]
@@ -243,7 +244,7 @@
         return e_ref.at[h * per_half + j, :, chunk_cols(k)]
 
     def unit(j, k):
-        return j if k is None else j + k
+        return j if k is None else whole + (j - whole) * CHUNKS + k
 
     def e_far(j, k=None):
         recv = e_recv.at[unit(j, k), z]
@@ -279,10 +280,11 @@
         arrived(ebuf.at[:, z_in * CORES + other], n_sems.at[1])
 
     def all_units(act):
-        for j in range(last):
+        for j in range(whole):
             act(j, None)
-        for k in range(CHUNKS):
-            act(last, k)
+        for j in range(whole, per_half):
+            for k in range(CHUNKS):
+                act(j, k)
 
     def partial_copy():
         return copy(pbuf, qbuf, p_send.at[0], p_recv.at[0], z_in, other)
@@ -298,20 +300,20 @@
             left, right, NT, preferred_element_type=jnp.float32
         ).astype(jnp.bfloat16).reshape(side, quarter, rows)
 
-    def project_last(q, k):
+    def project_part(j, q, k):
         at = pl.ds(pl.multiple_of(q * quarter, 16), quarter)
         cols, width = chunk_cols(k), chunks[k][1]
         left = wbuf[:, at, cols].reshape(side * quarter, width)
-        right = ebuf[last, :, :, cols].reshape(rows, width)
+        right = ebuf[j, :, :, cols].reshape(rows, width)
         total = lax.dot_general(
             left, right, NT, preferred_element_type=jnp.float32
         ).reshape(side, quarter, rows)
         if k > 0:
-            total = zsum[:, at] + total
+            total = zsum[j - whole, :, at] + total
         if k < CHUNKS - 1:
-            zsum[:, at] = total
+            zsum[j - whole, :, at] = total
         else:
-            zt[last, :, at] = total.astype(jnp.bfloat16)
+            zt[j, :, at] = total.astype(jnp.bfloat16)
 
     mine_at = pl.multiple_of(core * half_rows, half_rows)
     theirs_at = pl.multiple_of(other * half_rows, half_rows)
@@ -410,7 +412,6 @@
                 fold_core()
             for i in range(count):
                 outer_w(i, v).start()
-            each_mask()
             outer_diag(v).start()
 
             def send(j, k):
@@ -418,6 +419,7 @@
                 e_far(j, k).start()
 
             all_units(send)
+            each_mask()
 
     @pl.when(jnp.logical_and(inner, near))
     def _():
@@ -425,7 +427,6 @@
         fold_core()
         for i in range(count):
             far_w(i, 0).start()
-        each_mask()
         for j in range(per_half):
             near_e(j).start()
         own_g().wait()
@@ -438,6 +439,7 @@
                 to_far(w, i)
                 spread(w, i)
         all_units(lambda j, k: e_far(j, k).start())
+        each_mask()
         block, cols = weights(half, True, 1)
         arrived(wbuf.at[block, :, cols], g_recv.at[2])
         have_own()
@@ -463,22 +465,33 @@
                     got_diag(w)
                 fold(d_part, 0, direct)
 
-            @pl.when(t == last * PARTS - 3)
-            def _():
-                take_e(last, 0)
             project(choose(s, quarters), j)
 
             @pl.when(s == PARTS - 1)
             def _():
                 held_raw[j] = raw_scores(j, core, zt)
 
-        loop(last * PARTS, turn)
-
+        loop(whole * PARTS, turn)
+        take_e(whole, 0)
+        have_e(whole, 0)
+
+        def with_take(j, k, at):
+            def run(s):
+                @pl.when(s == at)
+                def _():
+                    take_e(whole + (k + 1) // CHUNKS, (k + 1) % CHUNKS)
+                project_part(j, choose(s, quarters), k)
+
+            loop(PARTS, run)
+
+        with_take(whole, 0, 3)
+        have_e(whole, 1)
+        with_take(whole, 1, 2)
+        held_raw[whole] = raw_scores(whole, core, zt)
+        take_e(last, 1)
         for k in range(CHUNKS):
-            if k + 1 < CHUNKS:
-                take_e(last, k + 1)
             have_e(last, k)
-            loop(PARTS, lambda s: project_last(choose(s, quarters), k))
+            loop(PARTS, lambda s: project_part(last, choose(s, quarters), k))
         loop(last, score_all)
         score_last()
         finish_last()
@@ -489,7 +502,6 @@
         near_g().start()
         for i in range(count):
             far_w(i, 1).start()
-        each_mask()
         near_w().start()
         for j in range(per_half):
             near_e(j).start()
@@ -499,13 +511,17 @@
                     got_mine(w, i)
                     spread(w, i)
         all_units(lambda j, k: e_far(j, k).start())
+        each_mask()
         for i in range(count):
             for v in range(2):
                 relay(inner_set[v], v, i)
         have_own()
         take_e(0)
         have_e(0)
-        order = ((0, 0), (1, 0), (2, 0), (0, 1), (1, 1), (2, 1), (0, 2), (1, 2), (2, 2), (3, 0), (3, 1), (3, 2))
+        order = ((0, 0), (1, 0), (2, 0), (0, 1), (1, 1), (2, 1), (3, 0), (3, 1))
+
+        def three_parts(j, k):
+            loop(PARTS - 1, lambda s: project_part(j, choose(s, quarters), k))
 
         def turn(t):
             what = choose(t, [q * PARTS + j for q, j in order])
@@ -522,29 +538,36 @@
             def _():
                 have_e(1)
 
+            @pl.when(t == 5)
+            def _():
+                take_e(whole, 0)
+
             @pl.when(t == 6)
             def _():
-                take_e(2)
-                have_e(2)
-
-            @pl.when(t == 9)
-            def _():
+                have_e(whole, 0)
+                three_parts(whole, 0)
+                take_e(whole, 1)
+                have_e(whole, 1)
+                three_parts(whole, 1)
                 take_e(last, 0)
                 have_e(last, 0)
-                loop(PARTS - 1, lambda s: project_last(choose(s, quarters), 0))
+                three_parts(last, 0)
                 for w in inner_set + outer_set:
                     got_diag(w)
                 take_e(last, 1)
             project(choose(what // PARTS, quarters), what % PARTS)
 
-            @pl.when(t >= 9)
-            def _():
-                far_copy(t - 9).start()
+            @pl.when(t >= 6)
+            def _():
+                far_copy(t - 6).start()
 
         loop(len(order), turn)
-        project_last(d_part, 0)
+        for k in range(CHUNKS):
+            project_part(whole, d_part, k)
+        far_copy(whole).start()
+        project_part(last, d_part, 0)
         have_e(last, 1)
-        loop(PARTS, lambda s: project_last(choose(s, quarters), 1))
+        loop(PARTS, lambda s: project_part(last, choose(s, quarters), 1))
         score_last()
         finish_last()
 
@@ -634,7 +657,7 @@
     per_half = prompts // 2
     rows = group * block_rows
     half_rows = rows // 2
-    units = per_half - 1 + CHUNKS
+    units = per_half - 2 + 2 * CHUNKS
     chip_width = features // CHIPS
     cut = held // 128 * 128
     bf16, f32 = jnp.bfloat16, jnp.float32
@@ -657,7 +680,7 @@
             pltpu.VMEM((chip_width - cut, cut), bf16),
             pltpu.VMEM((per_half, side, held, rows), bf16),
             pltpu.VMEM((per_half - 1, side, held, rows), bf16),
-            pltpu.VMEM((side, held, rows), f32),
+            pltpu.VMEM((2, side, held, rows), f32),
             pltpu.VMEM((per_half - 1, rows, rows), f32),
             pltpu.VMEM((rows, rows), f32),
             pltpu.VMEM((half_rows, rows), f32),
@@ -695,7 +718,7 @@
         compiler_params=pltpu.CompilerParams(
             collective_id=0, has_side_effects=True, vmem_limit_bytes=53 << 20
         ),
-    )(embeddings, head_weight, mask)
+    )(embeddings, head_weight, pltpu.with_memory_space_constraint(mask, pltpu.HBM))
 
 
 def shards(embeddings, head_weight, valid_mask):

time: 91 us -> 90.4 us (level)
    unnamed x4 -> x2, local copies, waits for them, and re-layouts: 1.98 us -> 1.3 us
where the time goes in v6:
time: 90.4 us; the launch traced here: 90.2 us
  Pallas kernels  88.3 us (98%)
  local copies, waits for them, and re-layouts  1.3 us (1%)
    pallas_call x1, Pallas kernels, line_scores(): pl.pallas_call(kernel, out_shape=(jax.ShapeDtypeStruct((prompts, block_ro...  88.3 us

profile of v6, /device:TPU:0, one launch (start us, length us, event | category | flops | bytes accessed | tf_op | source)
XLA Modules:
  0.0 90.2 jit_solution(8513475569271221107)
XLA Ops:
  0.6 88.3 %shard_map.50 = (f32[8,32,256]{2,1,0:T(8,128)S(1)}, f32[8,32]{1,0:T(8,128)S(1)}) custom-call(bf16[8,32,3584]{2,1,0:T(8,128)(2,1)} %e_ref.1, bf16[448,3584]{1,0:T(8,128)(2,1)} %w_ref.1, s32[8,32]{1,0:T(8,128)} %m_hbm.1), custom_call_target="tpu_custom_call" | custom-call | tf_op jit(solution)/shard_map/pallas_call | solution.py:667
  88.9 0.7 copy.7
  89.6 0.6 copy.8

commit v7 on v6

--- a/solution.py
+++ b/solution.py
@@ -50,9 +50,9 @@
 
 
 def kernel(e_ref, w_ref, m_hbm, o_ref, r_ref,
-           m_ref, ebuf, wbuf, gbuf, cbuf, zt, zfar, zsum, held_raw, sbuf, keep, pbuf, qbuf, fbuf, tbuf, rbuf, mine, mbuf,
+           m_ref, ebuf, wbuf, gbuf, cbuf, zt, zfar, zsum, held_raw, fbuf, tbuf, rbuf, lbuf, mine, mbuf,
            m_sems, e_send, e_recv, h_recv, n_sems, h_send, o_send, l_sems, g_send, g_recv,
-           x_send, y_send, u_send, v_send, a_recv, b_recv, d_recv, z_send, z_recv, p_send, p_recv, r_send, r_recv):
+           x_send, y_send, u_send, v_send, a_recv, b_recv, d_recv, z_send, z_recv, r_send, r_recv, s_recv):
     part = lax.axis_index("prompt")
     me = lax.axis_index("resp")
     z = me // CORES
@@ -65,7 +65,6 @@
     side = group // 2
     span = held * side
     rows = group * block_rows
-    half_rows = rows // 2
     quarter = held // PARTS
     z_in = 1 + half
     z_out = 3 * half
@@ -286,9 +285,6 @@
             for k in range(CHUNKS):
                 act(j, k)
 
-    def partial_copy():
-        return copy(pbuf, qbuf, p_send.at[0], p_recv.at[0], z_in, other)
-
     def far_copy(j):
         return copy(zt.at[j], zfar.at[j], z_send.at[0], z_recv.at[j], z_in, other)
 
@@ -299,6 +295,15 @@
         zt[j, :, at] = lax.dot_general(
             left, right, NT, preferred_element_type=jnp.float32
         ).astype(jnp.bfloat16).reshape(side, quarter, rows)
+
+    def project_pair(j, base):
+        at = pl.ds(pl.multiple_of(d_part * quarter, 16), quarter)
+        blocks = pl.ds(base, 2)
+        left = wbuf[blocks, at].reshape(2 * quarter, features)
+        right = ebuf[j].reshape(rows, features)
+        zt[j, blocks, at] = lax.dot_general(
+            left, right, NT, preferred_element_type=jnp.float32
+        ).astype(jnp.bfloat16).reshape(2, quarter, rows)
 
     def project_part(j, q, k):
         at = pl.ds(pl.multiple_of(q * quarter, 16), quarter)
@@ -315,28 +320,17 @@
         else:
             zt[j, :, at] = total.astype(jnp.bfloat16)
 
-    mine_at = pl.multiple_of(core * half_rows, half_rows)
-    theirs_at = pl.multiple_of(other * half_rows, half_rows)
-
     def raw_scores(j, c, held_zt):
         lanes = pl.ds(pl.multiple_of(c * span, 128), span)
         left = ebuf[j, :, :, lanes].reshape(rows, span)
         return jnp.dot(left, held_zt[j].reshape(span, rows), preferred_element_type=jnp.float32)
 
-    def score_last():
-        raw = raw_scores(last, core, zt)
-        sbuf[...] = raw - jnp.transpose(raw)
-        pbuf[...] = sbuf[pl.ds(theirs_at, half_rows)]
-        partial_copy().start()
-        keep[...] = sbuf[pl.ds(mine_at, half_rows)]
-
     def block_at(t):
         return pl.ds(pl.multiple_of(t * block_rows, block_rows), block_rows)
 
-    def final_copy(src, j, t):
+    def final_copy(src, dst, send, recv, t):
         return pltpu.make_async_remote_copy(
-            src, rbuf.at[half * per_half + j], r_send.at[0], r_recv.at[half, j // last],
-            device_id=(part, t), device_id_type=MESH,
+            src, dst, send, recv, device_id=(part, t), device_id_type=MESH
         )
 
     def score_all(j):
@@ -344,20 +338,17 @@
         raw = held_raw[j] + raw_scores(j, other, zfar)
         fbuf[j] = (raw - jnp.transpose(raw)).astype(jnp.bfloat16)
         for d in range(group - 1):
-            final_copy(fbuf.at[j, block_at(others[d])], j, others[d]).start()
-        rbuf[half * per_half + j] = fbuf[j, block_at(me)]
-
-    def finish_last():
-        arrived(qbuf, p_recv.at[0])
-        tbuf[...] = (keep[...] + qbuf[...]).astype(jnp.bfloat16)
-        for t in range(side):
-            @pl.when(core * side + t != me)
-            def _():
-                final_copy(tbuf.at[block_at(t)], last, core * side + t).start()
-
-        @pl.when(near)
-        def _():
-            rbuf[half * per_half + last] = tbuf[block_at(here)]
+            spot = rbuf.at[half * last + j]
+            final_copy(fbuf.at[j, block_at(others[d])], spot, r_send.at[0], r_recv.at[half], others[d]).start()
+        rbuf[half * last + j] = fbuf[j, block_at(me)]
+
+    def score_last():
+        raw = raw_scores(last, core, zt)
+        tbuf[...] = (raw - jnp.transpose(raw)).astype(jnp.bfloat16)
+        for d in range(group - 1):
+            spot = lbuf.at[half, core]
+            final_copy(tbuf.at[block_at(others[d])], spot, r_send.at[1], s_recv.at[half, core], others[d]).start()
+        lbuf[half, core] = tbuf[block_at(me)]
 
     def each_mask():
         for d in range(group - 1):
@@ -492,9 +483,8 @@
         for k in range(CHUNKS):
             have_e(last, k)
             loop(PARTS, lambda s: project_part(last, choose(s, quarters), k))
+        score_last()
         loop(last, score_all)
-        score_last()
-        finish_last()
 
     @pl.when(jnp.logical_and(inner, jnp.logical_not(near)))
     def _():
@@ -518,7 +508,7 @@
         have_own()
         take_e(0)
         have_e(0)
-        order = ((0, 0), (1, 0), (2, 0), (0, 1), (1, 1), (2, 1), (3, 0), (3, 1))
+        order = ((0, 0), (1, 0), (2, 0), (0, 1), (1, 1), (2, 1))
 
         def three_parts(j, k):
             loop(PARTS - 1, lambda s: project_part(j, choose(s, quarters), k))
@@ -542,26 +532,29 @@
             def _():
                 take_e(whole, 0)
 
-            @pl.when(t == 6)
-            def _():
-                have_e(whole, 0)
-                three_parts(whole, 0)
-                take_e(whole, 1)
-                have_e(whole, 1)
-                three_parts(whole, 1)
-                take_e(last, 0)
-                have_e(last, 0)
-                three_parts(last, 0)
-                for w in inner_set + outer_set:
-                    got_diag(w)
-                take_e(last, 1)
             project(choose(what // PARTS, quarters), what % PARTS)
 
-            @pl.when(t >= 6)
-            def _():
-                far_copy(t - 6).start()
-
         loop(len(order), turn)
+        have_e(whole, 0)
+        three_parts(whole, 0)
+        take_e(whole, 1)
+        for w in inner_set:
+            got_diag(w)
+        loop(whole, lambda j: project_pair(j, 2 * (1 - core)))
+        have_e(whole, 1)
+        three_parts(whole, 1)
+        take_e(last, 0)
+        have_e(last, 0)
+        three_parts(last, 0)
+        for w in outer_set:
+            got_diag(w)
+        take_e(last, 1)
+
+        def diag_turn(j):
+            project_pair(j, 2 * core)
+            far_copy(j).start()
+
+        loop(whole, diag_turn)
         for k in range(CHUNKS):
             project_part(whole, d_part, k)
         far_copy(whole).start()
@@ -569,7 +562,6 @@
         have_e(last, 1)
         loop(PARTS, lambda s: project_part(last, choose(s, quarters), 1))
         score_last()
-        finish_last()
 
     arrived(mbuf.at[pl.ds(0, group - 1)], m_sems.at[1])
     mbuf[me] = mine[...]
@@ -585,19 +577,32 @@
     down = lax.dot_general(same, valid, NT, preferred_element_type=jnp.float32)
     lane = lax.broadcasted_iota(jnp.int32, (block_rows, 128), 1)
     rates = jnp.zeros((block_rows, 128), jnp.float32)
-    for batch in (range(last), range(last, per_half)):
-        for h in range(2):
-            @pl.when(jnp.logical_not(jnp.logical_and(jnp.logical_and(inner, near), half == h)))
-            def _():
-                arrived(rbuf.at[pl.ds(h * per_half + batch[0], len(batch))], r_recv.at[h, batch[0] // last])
-        for j in batch:
-            for h in range(2):
-                p = h * per_half + j
-                given = down[:, p:p + 1]
-                prefs = jax.nn.sigmoid(rbuf[p].astype(jnp.float32)) * given * cols[p:p + 1, :]
-                o_ref[p] = prefs
-                totals = jnp.sum(prefs, axis=1, keepdims=True) - 0.5 * given
-                rates = jnp.where(lane == p, given * totals / pairs[p:p + 1, :], rates)
+    def settle(p, scores, rates):
+        given = down[:, p:p + 1]
+        prefs = jax.nn.sigmoid(scores) * given * cols[p:p + 1, :]
+        o_ref[p] = prefs
+        totals = jnp.sum(prefs, axis=1, keepdims=True) - 0.5 * given
+        return jnp.where(lane == p, given * totals / pairs[p:p + 1, :], rates)
+
+    for h in range(2):
+        at_home = jnp.logical_and(inner, half == h)
+
+        @pl.when(jnp.logical_not(jnp.logical_and(at_home, near)))
+        def _():
+            arrived(rbuf.at[pl.ds(h * last, last)], r_recv.at[h])
+    for h in range(2):
+        for j in range(last):
+            rates = settle(h * per_half + j, rbuf[h * last + j].astype(jnp.float32), rates)
+    for h in range(2):
+        for c in range(CORES):
+            at_home = jnp.logical_and(inner, half == h)
+
+            @pl.when(jnp.logical_not(jnp.logical_and(at_home, core == c)))
+            def _():
+                arrived(lbuf.at[h, c], s_recv.at[h, c])
+    for h in range(2):
+        scores = lbuf[h, 0].astype(jnp.float32) + lbuf[h, 1].astype(jnp.float32)
+        rates = settle(h * per_half + last, scores, rates)
     r_ref[...] = jnp.transpose(rates)[:prompts]
 
     departed(mbuf.at[pl.ds(0, group - 1)], m_sems.at[0])
@@ -628,7 +633,6 @@
     def _():
         departed(ebuf.at[:, 0], n_sems.at[0])
         departed(ebuf.at[:, pl.ds(0, 3)], h_send.at[0])
-        departed(pbuf, p_send.at[0])
 
     @pl.when(jnp.logical_and(inner, near))
     def _():
@@ -636,7 +640,8 @@
             for sems in (x_send, y_send, u_send):
                 sent_rows(w, sems, quarter)
             sent_rows(w, v_send, quarter - direct)
-        departed(fbuf, r_send.at[0])
+        departed(fbuf.at[:, pl.ds(0, rows - block_rows)], r_send.at[0])
+        departed(tbuf.at[pl.ds(0, rows - block_rows)], r_send.at[1])
 
     @pl.when(jnp.logical_and(inner, jnp.logical_not(near)))
     def _():
@@ -646,7 +651,7 @@
             for sems in (x_send, y_send, v_send):
                 sent_rows(w, sems, quarter)
         departed(zt.at[pl.ds(0, last)], z_send.at[0])
-        departed(tbuf, r_send.at[0])
+        departed(tbuf.at[pl.ds(0, rows - block_rows)], r_send.at[1])
 
 
 def line_scores(embeddings, head_weight, mask):
@@ -656,7 +661,6 @@
     side = group // 2
     per_half = prompts // 2
     rows = group * block_rows
-    half_rows = rows // 2
     units = per_half - 2 + 2 * CHUNKS
     chip_width = features // CHIPS
     cut = held // 128 * 128
@@ -682,13 +686,10 @@
             pltpu.VMEM((per_half - 1, side, held, rows), bf16),
             pltpu.VMEM((2, side, held, rows), f32),
             pltpu.VMEM((per_half - 1, rows, rows), f32),
-            pltpu.VMEM((rows, rows), f32),
-            pltpu.VMEM((half_rows, rows), f32),
-            pltpu.VMEM((half_rows, rows), f32),
-            pltpu.VMEM((half_rows, rows), f32),
             pltpu.VMEM((per_half - 1, rows, rows), bf16),
-            pltpu.VMEM((half_rows, rows), bf16),
-            pltpu.VMEM((prompts, block_rows, rows), bf16),
+            pltpu.VMEM((rows, rows), bf16),
+            pltpu.VMEM((prompts - 2, block_rows, rows), bf16),
+            pltpu.VMEM((2, CORES, block_rows, rows), bf16),
             pltpu.VMEM((prompts, 128), jnp.int32),
             pltpu.VMEM((group, prompts, 128), jnp.int32),
             dma((3,)),
@@ -710,10 +711,9 @@
             dma((side,)),
             dma((1,)),
             dma((per_half - 1,)),
-            dma((1,)),
-            dma((1,)),
-            dma((1,)),
-            dma((2, 2)),
+            dma((2,)),
+            dma((2,)),
+            dma((2, CORES)),
         ],
         compiler_params=pltpu.CompilerParams(
             collective_id=0, has_side_effects=True, vmem_limit_bytes=53 << 20

time: 90.4 us -> 88.8 us (0.982)
  Pallas kernels: 88.3 us -> 86.6 us
    pallas_call x1, Pallas kernels: 88.3 us -> 86.6 us  [line_scores(): pl.pallas_call(kernel, out_shape=(jax.ShapeDtypeStruct((prompts, block_ro...]
where the time goes in v7:
time: 88.8 us; the launch traced here: 88.6 us
  Pallas kernels  86.6 us (98%)
  local copies, waits for them, and re-layouts  1.3 us (1%)
    pallas_call x1, Pallas kernels, line_scores(): pl.pallas_call(kernel, out_shape=(jax.ShapeDtypeStruct((prompts, block_ro...  86.6 us

profile of v7, /device:TPU:0, one launch (start us, length us, event | category | flops | bytes accessed | tf_op | source)
XLA Modules:
  0.0 88.6 jit_solution(11448691093536980717)
XLA Ops:
  0.6 86.6 %shard_map.50 = (f32[8,32,256]{2,1,0:T(8,128)S(1)}, f32[8,32]{1,0:T(8,128)S(1)}) custom-call(bf16[8,32,3584]{2,1,0:T(8,128)(2,1)} %e_ref.1, bf16[448,3584]{1,0:T(8,128)(2,1)} %w_ref.1, s32[8,32]{1,0:T(8,128)} %m_hbm.1), custom_call_target="tpu_custom_call" | custom-call | tf_op jit(solution)/shard_map/pallas_call | solution.py:671
  87.3 0.7 copy.7
  88.0 0.6 copy.8

commit v8 on v7

--- a/solution.py
+++ b/solution.py
@@ -52,7 +52,7 @@
 def kernel(e_ref, w_ref, m_hbm, o_ref, r_ref,
            m_ref, ebuf, wbuf, gbuf, cbuf, zt, zfar, zsum, held_raw, fbuf, tbuf, rbuf, lbuf, mine, mbuf,
            m_sems, e_send, e_recv, h_recv, n_sems, h_send, o_send, l_sems, g_send, g_recv,
-           x_send, y_send, u_send, v_send, a_recv, b_recv, d_recv, z_send, z_recv, r_send, r_recv, s_recv):
+           w_send, a_recv, b_recv, d_recv, z_send, z_recv, r_send, r_recv, s_recv):
     part = lax.axis_index("prompt")
     me = lax.axis_index("resp")
     z = me // CORES
@@ -212,22 +212,22 @@
         return copy(spot, spot, send, recv, chip, core, q_to)
 
     def spread(w, i):
-        along(w, part, i, x_send.at[w[0]], b_recv.at[w[0], i], z_in, x_part).start()
-        along(w, part, i, y_send.at[w[0]], b_recv.at[w[0], i], z_in, y_part).start()
+        along(w, part, i, w_send.at[w[0]], b_recv.at[w[0], i], z_in, x_part).start()
+        along(w, part, i, w_send.at[w[0]], b_recv.at[w[0], i], z_in, y_part).start()
 
     def to_far(w, i):
-        along(w, part, i, u_send.at[w[0]], a_recv.at[w[0], i], z_far, part).start()
+        along(w, part, i, w_send.at[w[0]], a_recv.at[w[0], i], z_far, part).start()
 
     def relay(w, v, i):
         got_sides(w, i)
         if (i < 2) == (v == 0):
-            along(w, x_part, i, v_send.at[w[0]], d_recv.at[w[0]], z_in, y_part).start()
+            along(w, x_part, i, w_send.at[w[0]], d_recv.at[w[0]], z_in, y_part).start()
         else:
-            along(w, y_part, i, v_send.at[w[0]], d_recv.at[w[0]], z_in, x_part).start()
-
-    def sent_rows(w, send, many):
+            along(w, y_part, i, w_send.at[w[0]], d_recv.at[w[0]], z_in, x_part).start()
+
+    def sent_rows(w, many):
         block, cols = w
-        departed(wbuf.at[block, pl.ds(0, many), cols], send.at[block])
+        departed(wbuf.at[block, pl.ds(0, many), cols], w_send.at[block])
 
     def chunk_cols(k):
         return pl.ds(*chunks[k])
@@ -245,12 +245,15 @@
     def unit(j, k):
         return j if k is None else whole + (j - whole) * CHUNKS + k
 
+    def rank(chip, there):
+        return jnp.where(chip > there, chip - 1, chip)
+
     def e_far(j, k=None):
-        recv = e_recv.at[unit(j, k), z]
+        recv = e_recv.at[unit(j, k), rank(z, z_far)]
         return copy(e_mine(1 - half, j, k), e_part(j, me, k), e_send.at[1], recv, z_far, core)
 
     def e_near(j, k=None):
-        return copy(e_mine(half, j, k), e_part(j, me, k), e_send.at[0], e_recv.at[unit(j, k), z], z_in, core)
+        return copy(e_mine(half, j, k), e_part(j, me, k), e_send.at[0], e_recv.at[unit(j, k), rank(z, z_in)], z_in, core)
 
     def near_e(j):
         return copy(e_mine(half, j, None), ebuf.at[j, me], n_sems.at[0], n_sems.at[1], z_in, other)
@@ -268,7 +271,7 @@
     def take_e(j, k=None):
         for chip in away:
             spot = e_part(j, chip * CORES + core, k)
-            arrived(spot, e_recv.at[unit(j, k), chip])
+            arrived(spot, e_recv.at[unit(j, k), rank(chip, z_in)])
             copy(spot, spot, h_send.at[0], h_recv.at[unit(j, k)], z_in, other).start()
 
     def have_e(j, k=None):
@@ -555,12 +558,16 @@
             far_copy(j).start()
 
         loop(whole, diag_turn)
-        for k in range(CHUNKS):
-            project_part(whole, d_part, k)
-        far_copy(whole).start()
-        project_part(last, d_part, 0)
-        have_e(last, 1)
-        loop(PARTS, lambda s: project_part(last, choose(s, quarters), 1))
+        loop(2, lambda n: project_part(whole + n, d_part, 0))
+
+        def final_turn(n):
+            @pl.when(n == 1)
+            def _():
+                far_copy(whole).start()
+                have_e(last, 1)
+            project_part(jnp.where(n > 0, last, whole), choose(n, (d_part,) + quarters), 1)
+
+        loop(1 + PARTS, final_turn)
         score_last()
 
     arrived(mbuf.at[pl.ds(0, group - 1)], m_sems.at[1])
@@ -637,9 +644,7 @@
     @pl.when(jnp.logical_and(inner, near))
     def _():
         for w in outer_set:
-            for sems in (x_send, y_send, u_send):
-                sent_rows(w, sems, quarter)
-            sent_rows(w, v_send, quarter - direct)
+            sent_rows(w, 4 * quarter - direct)
         departed(fbuf.at[:, pl.ds(0, rows - block_rows)], r_send.at[0])
         departed(tbuf.at[pl.ds(0, rows - block_rows)], r_send.at[1])
 
@@ -648,8 +653,7 @@
         near_g().wait_send()
         near_w().wait_send()
         for w in inner_set + outer_set:
-            for sems in (x_send, y_send, v_send):
-                sent_rows(w, sems, quarter)
+            sent_rows(w, 3 * quarter)
         departed(zt.at[pl.ds(0, last)], z_send.at[0])
         departed(tbuf.at[pl.ds(0, rows - block_rows)], r_send.at[1])
 
@@ -694,7 +698,7 @@
             pltpu.VMEM((group, prompts, 128), jnp.int32),
             dma((3,)),
             dma((2,)),
-            dma((units, CHIPS)),
+            dma((units, CHIPS - 1)),
             dma((units,)),
             dma((3,)),
             dma((1,)),
@@ -702,9 +706,6 @@
             dma((2,)),
             dma((3,)),
             dma((3,)),
-            dma((side,)),
-            dma((side,)),
-            dma((side,)),
             dma((side,)),
             dma((side, 4)),
             dma((side, 4)),

time: 88.8 us -> 88.5 us (level)
  no operation moved by 1% of the time
where the time goes in v8:
time: 88.5 us; the launch traced here: 88.3 us
  Pallas kernels  86.4 us (98%)
  local copies, waits for them, and re-layouts  1.3 us (1%)
    pallas_call x1, Pallas kernels, line_scores(): pl.pallas_call(kernel, out_shape=(jax.ShapeDtypeStruct((prompts, block_ro...  86.4 us

profile of v8, /device:TPU:0, one launch (start us, length us, event | category | flops | bytes accessed | tf_op | source)
XLA Modules:
  0.0 88.3 jit_solution(4393843392350658872)
XLA Ops:
  0.6 86.4 %shard_map.50 = (f32[8,32,256]{2,1,0:T(8,128)S(1)}, f32[8,32]{1,0:T(8,128)S(1)}) custom-call(bf16[8,32,3584]{2,1,0:T(8,128)(2,1)} %e_ref.1, bf16[448,3584]{1,0:T(8,128)(2,1)} %w_ref.1, s32[8,32]{1,0:T(8,128)} %m_hbm.1), custom_call_target="tpu_custom_call" | custom-call | tf_op jit(solution)/shard_map/pallas_call | solution.py:675
  87.0 0.7 copy.7
  87.7 0.6 copy.8
